TPU v7x, 256 devices: a whole 4x4x8 slice. The times are simulated.
256 devices in a mesh: lon: 16 (over y_hi, z), day: 16 (over x, y_lo, core).
Axes of the slice: x: 4, y: 4 (y_hi: 2, y_lo: 2; y = y_hi * 2 + y_lo), z: 8, core: 2. Of those that a mesh axis runs over, the one named last changes fastest.
Arguments:
- field: bfloat16 [368, 1440, 1024], P('day', 'lon'), may hold values from -6 to 6
Outputs:
- filtered: float32 [368, 1440, 1024], P('day', 'lon')
All inputs are finite; a program needn't handle non-finite values.
Results may differ from a plain program's by a relative error of at most 0.0003.
Values may be sent and summed in bfloat16 or wider, within the bound.
A program may use at most 192 MiB of HBM per device.

v0:
```python
import jax
import jax.numpy as jnp
from jax import lax
from jax.sharding import PartitionSpec as P

DAY_HALF = 15
LON_HALF = 10


def extended(cells, sides, width):
    for axis, dim in sides:
        count = lax.axis_size(axis)
        head = lax.slice_in_dim(cells, 0, width, axis=dim)
        tail = lax.slice_in_dim(cells, cells.shape[dim] - width, cells.shape[dim], axis=dim)
        cells = jnp.concatenate(
            [
                lax.ppermute(tail, axis, [(i, (i + 1) % count) for i in range(count)]),
                cells,
                lax.ppermute(head, axis, [((i + 1) % count, i) for i in range(count)]),
            ],
            axis=dim,
        )
    return cells


def running(values, dim, half):
    count = values.shape[dim] - 2 * half
    total = jnp.cumsum(values, axis=dim)
    first = jnp.zeros_like(lax.slice_in_dim(total, 0, 1, axis=dim))
    total = jnp.concatenate([first, total], axis=dim)
    upper = lax.slice_in_dim(total, 2 * half + 1, 2 * half + 1 + count, axis=dim)
    lower = lax.slice_in_dim(total, 0, count, axis=dim)
    return (upper - lower) / (2.0 * half + 1.0)


def local(field):
    tall = extended(field, (("day", 0),), DAY_HALF)
    values = tall.astype(jnp.float32)
    clim = running(values, 0, DAY_HALF)
    anomaly = values[DAY_HALF : values.shape[0] - DAY_HALF] - clim
    padded = extended(anomaly, (("lon", 1),), LON_HALF)
    return running(padded, 1, LON_HALF)


def solution(mesh):
    return jax.shard_map(
        local,
        mesh=mesh,
        in_specs=(P("day", "lon", None),),
        out_specs=P("day", "lon", None),
        check_vma=False,
    )
```

profile of v0, /device:TPU:1, one launch (start us, length us, event | category | flops | bytes accessed | tf_op | source)
XLA Modules:
  0.0 157.4 jit_solution(8249850145674973770)
XLA Ops:
  0.0 4.7 %copy.6 = bf16[23,90,1024]{2,1,0:T(8,128)(2,1)S(1)} copy(bf16[23,90,1024]{2,0,1:T(8,128)(2,1)} %param.1) | data formatting | bytes 8478720 | tf_op args[0]
  4.7 0.0 copy-start.1
  4.7 0.7 fusion.9
  5.5 2.8 %collective-permute-start = (bf16[15,90,1024]{2,1,0:T(8,128)(2,1)S(1)}, bf16[15,90,1024]{2,1,0:T(8,128)(2,1)S(1)}, u32[]{:S(2)}, u32[]{:S(2)}) collective-permute-start(bf16[15,90,1024]{2,1,0:T(8,128)(2,1)S(1)} %get-tuple-element.7), channel_id=1, source_target_pairs={{0,1},{1,2},{2,3},{3,4},{4,5},{5,6},{6,7},{7,8},{8,9},{9,10},{10,1... | collective-permute-start | bytes 8294408 | tf_op jit(solution)/shard_map/ppermute | solution.py:17
  8.2 0.6 collective-permute-start.1
  8.8 63.1 %collective-permute-done = bf16[15,90,1024]{2,1,0:T(8,128)(2,1)S(1)} collective-permute-done((bf16[15,90,1024]{2,1,0:T(8,128)(2,1)S(1)}, bf16[15,90,1024]{2,1,0:T(8,128)(2,1)S(1)}, u32[]{:S(2)}, u32[]{:S(2)}) %collective-permute-start) | collective-permute-done | bytes 2764832 | tf_op jit(solution)/shard_map/ppermute | solution.py:17
  71.9 2.6 %collective-permute-done.1 = bf16[15,90,1024]{2,1,0:T(8,128)(2,1)} collective-permute-done((bf16[15,90,1024]{2,1,0:T(8,128)(2,1)S(1)}, bf16[15,90,1024]{2,1,0:T(8,128)(2,1)}, u32[]{:S(2)}, u32[]{:S(2)}) %collective-permute-start.1) | collective-permute-done | bytes 2764832 | tf_op jit(solution)/shard_map/ppermute | solution.py:19
  74.5 0.0 copy-done.3
  74.5 8.7 %fusion.7 = f32[53,90,1024]{2,1,0:T(8,128)} fusion(bf16[15,90,1024]{2,1,0:T(8,128)(2,1)} %collective-permute-done.1, bf16[23,90,1024]{2,1,0:T(8,128)(2,1)S(1)} %copy.6, bf16[15,90,1024]{2,1,0:T(8,128)(2,1)S(1)} %collective-permute-done), kind=kOutput, calls=%fused_computation.11 | output fusion | flops 268646400 | bytes 29306880 | tf_op jit(solution)/shard_map/jit(cumsum)/reduce_window_sum | solution.py:28
  83.2 13.1 %maximum_convert_fusion = f32[53,90,1024]{2,1,0:T(8,128)} fusion(bf16[15,90,1024]{2,1,0:T(8,128)(2,1)} %collective-permute-done.1, bf16[23,90,1024]{2,1,0:T(8,128)(2,1)} %copy-done.1, bf16[15,90,1024]{2,1,0:T(8,128)(2,1)} %copy-done.3), kind=kLoop, calls=%fused_computation.5 | loop fusion | flops 14653440 | bytes 29306880 | tf_op jit(solution)/shard_map/convert_element_type | solution.py:38
  96.3 4.5 %copy-done = f32[53,90,1024]{2,1,0:T(8,128)S(1)} copy-done((f32[53,90,1024]{2,1,0:T(8,128)S(1)}, f32[53,90,1024]{2,1,0:T(8,128)}, u32[]{:S(2)}) %copy-start) | copy-done | bytes 19537944
  100.8 7.7 %fusion.4 = f32[23,90,1024]{2,1,0:T(8,128)} fusion(f32[53,90,1024]{2,1,0:T(8,128)S(1)} %copy-done, f32[53,90,1024]{2,1,0:T(8,128)} %maximum_convert_fusion), kind=kLoop, calls=%fused_computation.8 | loop fusion | flops 6359040 | bytes 46841856 | tf_op jit(solution)/shard_map/sub | solution.py:40
  108.5 2.2 %fusion.8 = (f32[23,10,1024]{2,1,0:T(8,128)S(1)}, f32[23,10,1024]{2,1,0:T(8,128)S(1)}) fusion(f32[23,90,1024]{2,1,0:T(8,128)} %fusion.4), kind=kLoop, calls=%fused_computation.12 | loop fusion | bytes 3768320 | tf_op jit(solution)/shard_map/slice | solution.py:14
  110.7 0.6 copy.10
  111.3 8.0 %collective-permute-start.3 = (f32[23,10,1024]{2,0,1:T(8,128)S(1)}, f32[23,10,1024]{2,0,1:T(8,128)S(1)}, u32[]{:S(2)}, u32[]{:S(2)}) collective-permute-start(f32[23,10,1024]{2,0,1:T(8,128)S(1)} %copy.10), channel_id=1, source_target_pairs={{16,0},{32,16},{48,32},{64,48},{80,64},{96,80},{112,96},{128,112},... | collective-permute-start | bytes 2826248 | tf_op jit(solution)/shard_map/ppermute | solution.py:19
  119.3 0.6 copy.9
  119.8 0.3 collective-permute-start.2
  120.1 10.2 %collective-permute-done.3 = f32[23,10,1024]{2,0,1:T(8,128)S(1)} collective-permute-done((f32[23,10,1024]{2,0,1:T(8,128)S(1)}, f32[23,10,1024]{2,0,1:T(8,128)S(1)}, u32[]{:S(2)}, u32[]{:S(2)}) %collective-permute-start.3) | collective-permute-done | bytes 942112 | tf_op jit(solution)/shard_map/ppermute | solution.py:19
  130.3 0.6 copy.12
  130.9 5.7 %collective-permute-done.2 = f32[23,10,1024]{2,0,1:T(8,128)S(1)} collective-permute-done((f32[23,10,1024]{2,0,1:T(8,128)S(1)}, f32[23,10,1024]{2,0,1:T(8,128)S(1)}, u32[]{:S(2)}, u32[]{:S(2)}) %collective-permute-start.2) | collective-permute-done | bytes 942112 | tf_op jit(solution)/shard_map/ppermute | solution.py:17
  136.7 0.6 copy.11
  137.2 4.8 %pad_maximum_fusion = f32[23,110,1024]{2,1,0:T(8,128)} fusion(f32[23,10,1024]{2,1,0:T(8,128)S(1)} %copy.12, f32[23,90,1024]{2,1,0:T(8,128)S(1)} %copy-done.2, f32[23,10,1024]{2,1,0:T(8,128)S(1)} %copy.11), kind=kLoop, calls=%fused_computation.4 | loop fusion | flops 5181440 | bytes 20725760 | tf_op jit(solution)/shard_map/concatenate | solution.py:15
  142.1 10.7 %fusion = f32[23,110,1024]{2,0,1:T(8,128)S(1)} fusion(f32[23,110,1024]{2,1,0:T(8,128)} %pad_maximum_fusion), kind=kOutput, calls=%fused_computation.2 | output fusion | flops 282388480 | bytes 20725760 | tf_op jit(solution)/shard_map/jit(cumsum)/reduce_window_sum | solution.py:28
  152.7 4.6 %fusion.6 = f32[23,90,1024]{2,0,1:T(8,128)} fusion(f32[23,110,1024]{2,0,1:T(8,128)S(1)} %fusion), kind=kLoop, calls=%fused_computation.10 | loop fusion | flops 4239360 | bytes 28139520 | tf_op jit(solution)/shard_map/div | solution.py:33
  (5 shorter events, 0.0 us)
Async XLA Ops:
  4.7 69.8 %copy-start.1 = (bf16[23,90,1024]{2,1,0:T(8,128)(2,1)}, bf16[23,90,1024]{2,1,0:T(8,128)(2,1)S(1)}, u32[]{:S(2)}) copy-start(bf16[23,90,1024]{2,1,0:T(8,128)(2,1)S(1)} %copy.6) | copy-start | bytes 12718084
  5.5 66.5 %collective-permute-start = (bf16[15,90,1024]{2,1,0:T(8,128)(2,1)S(1)}, bf16[15,90,1024]{2,1,0:T(8,128)(2,1)S(1)}, u32[]{:S(2)}, u32[]{:S(2)}) collective-permute-start(bf16[15,90,1024]{2,1,0:T(8,128)(2,1)S(1)} %get-tuple-element.7), channel_id=1, source_target_pairs={{0,1},{1,2},{2,3},{3,4},{4,5},{5,6},{6,7},{7,8},{8,9},{9,10},{10,1... | collective-permute-start | bytes 8294408 | tf_op jit(solution)/shard_map/ppermute | solution.py:17
  8.2 66.3 %collective-permute-start.1 = (bf16[15,90,1024]{2,1,0:T(8,128)(2,1)S(1)}, bf16[15,90,1024]{2,1,0:T(8,128)(2,1)}, u32[]{:S(2)}, u32[]{:S(2)}) collective-permute-start(bf16[15,90,1024]{2,1,0:T(8,128)(2,1)S(1)} %get-tuple-element.8), channel_id=1, source_target_pairs={{1,0},{2,1},{3,2},{4,3},{5,4},{6,5},{7,6},{8,7},{9,8},{10,9},{11,1... | collective-permute-start | bytes 8294408 | tf_op jit(solution)/shard_map/ppermute | solution.py:19
  71.9 2.6 %copy-start.3 = (bf16[15,90,1024]{2,1,0:T(8,128)(2,1)}, bf16[15,90,1024]{2,1,0:T(8,128)(2,1)S(1)}, u32[]{:S(2)}) copy-start(bf16[15,90,1024]{2,1,0:T(8,128)(2,1)S(1)} %collective-permute-done) | copy-start | bytes 8294404
  83.2 17.6 %copy-start = (f32[53,90,1024]{2,1,0:T(8,128)S(1)}, f32[53,90,1024]{2,1,0:T(8,128)}, u32[]{:S(2)}) copy-start(f32[53,90,1024]{2,1,0:T(8,128)} %fusion.7) | copy-start | bytes 58613764
  108.5 28.7 %copy-start.2 = (f32[23,90,1024]{2,1,0:T(8,128)S(1)}, f32[23,90,1024]{2,1,0:T(8,128)}, u32[]{:S(2)}) copy-start(f32[23,90,1024]{2,1,0:T(8,128)} %fusion.4) | copy-start | bytes 25436164
  111.3 19.0 %collective-permute-start.3 = (f32[23,10,1024]{2,0,1:T(8,128)S(1)}, f32[23,10,1024]{2,0,1:T(8,128)S(1)}, u32[]{:S(2)}, u32[]{:S(2)}) collective-permute-start(f32[23,10,1024]{2,0,1:T(8,128)S(1)} %copy.10), channel_id=1, source_target_pairs={{16,0},{32,16},{48,32},{64,48},{80,64},{96,80},{112,96},{128,112},... | collective-permute-start | bytes 2826248 | tf_op jit(solution)/shard_map/ppermute | solution.py:19
  119.8 16.8 %collective-permute-start.2 = (f32[23,10,1024]{2,0,1:T(8,128)S(1)}, f32[23,10,1024]{2,0,1:T(8,128)S(1)}, u32[]{:S(2)}, u32[]{:S(2)}) collective-permute-start(f32[23,10,1024]{2,0,1:T(8,128)S(1)} %copy.9), channel_id=1, source_target_pairs={{0,16},{16,32},{32,48},{48,64},{64,80},{80,96},{96,112},{112,128},... | collective-permute-start | bytes 2826248 | tf_op jit(solution)/shard_map/ppermute | solution.py:17
where the time goes:
time: 158 us; the launch traced here: 157 us
  waiting for transfers between devices  81.6 us (52%)
  other arithmetic  49.6 us (31%)
  local copies, waits for them, and re-layouts  14.4 us (9%)
  starting transfers between devices  11.6 us (7%)
    ppermute x2, waiting for transfers between devices, extended(): lax.ppermute(tail, axis, [(i, (i + 1) % count) for i in range(count)])  68.8 us
    another operation x2, other arithmetic, running(): total = jnp.cumsum(values, axis=dim)  19.4 us
    convert_element_type x1, other arithmetic, local(): values = tall.astype(jnp.float32)  13.1 us
    ppermute x2, waiting for transfers between devices, extended(): lax.ppermute(head, axis, [((i + 1) % count, i) for i in range(count)])  12.8 us
    unnamed x9, local copies, waits for them, and re-layouts  9.21 us
    ppermute x2, starting transfers between devices, extended(): lax.ppermute(head, axis, [((i + 1) % count, i) for i in range(count)])  8.6 us
    sub x1, other arithmetic, local(): anomaly = values[DAY_HALF:values.shape[0] - DAY_HALF] - clim  7.71 us
    concatenate x1, other arithmetic, extended(): jnp.concatenate([lax.ppermute(tail, axis, [(i, (i + 1) % count) for i in...  4.81 us
  transfers between devices with their start and end apart: 4, of which 4 were waited for; matrix products, arithmetic and copies ran while one was open for 1% of the time, Pallas kernels for 0%

commit v1 on v0

v1 whole, which is shorter than its diff:
```python
import functools

import jax
import jax.numpy as jnp
import numpy as np
from jax import lax
from jax.experimental import pallas as pl
from jax.experimental.pallas import tpu as pltpu
from jax.sharding import PartitionSpec as P

DAY_HALF = 15
LON_HALF = 10
PLANES = 8
STEP = 10
TILE = 8
MESH = pl.DeviceIdType.MESH


def kernel(lons, days, field, tail, weights, out, own, near, far, terms, done, local_sem, send, recv, out_sem):
    count = field.shape[0]
    here = lax.axis_index("lon")
    day = lax.axis_index("day")
    core = lax.rem(day, 2)
    turn = 2 * core - 1
    far_day = lax.rem(day + turn + days, days)
    near_day = lax.rem(day - turn + days, days)
    east = lax.rem(here + 1, lons)
    west = lax.rem(here + lons - 1, lons)
    plane = lax.rem(here, PLANES)
    edge = LON_HALF
    wide = count + 2 * edge

    rows = pl.ds(pl.multiple_of(TILE * core, TILE), TILE)
    head_rows, tail_rows = pl.ds(0, TILE), pl.ds(TILE, TILE)

    partners = ((here, far_day), (here, near_day), (east, day), (west, day), (east, far_day), (west, far_day))
    barrier = pltpu.get_barrier_semaphore()
    for partner in partners:
        pl.semaphore_signal(barrier, inc=1, device_id=partner, device_id_type=MESH)
    load = pltpu.make_async_copy(field, own.at[pl.ds(edge, count)], local_sem)
    load.start()
    pl.semaphore_wait(barrier, len(partners))

    def remote(source, target, slot, device):
        return pltpu.make_async_remote_copy(
            src_ref=source, dst_ref=target, send_sem=send.at[slot], recv_sem=recv.at[slot],
            device_id=device, device_id_type=MESH,
        )

    chunks = (count - 2 * edge) // STEP
    low, high = pl.ds(0, edge), pl.ds(count - edge, edge)
    first, last = pl.ds(edge, edge), pl.ds(count, edge)
    before, after = pl.ds(0, edge), pl.ds(count + edge, edge)

    def pair(lon_span, target_span, slot, device):
        return (
            remote(field.at[lon_span, rows], far.at[target_span, head_rows], slot, device),
            remote(tail.at[lon_span], far.at[target_span, tail_rows], slot + 1, device),
        )

    to_east = remote(field.at[high], own.at[before], 0, (east, day))
    to_west = remote(field.at[low], own.at[after], 1, (west, day))
    far_edges = pair(low, first, 2, (here, far_day)) + pair(high, last, 4, (here, far_day))
    near_all = remote(field, near.at[pl.ds(edge, count)], 6, (here, near_day))
    near_before = remote(own.at[before], near.at[before], 7, (here, near_day))
    near_after = remote(own.at[after], near.at[after], 8, (here, near_day))
    east_direct = pair(high, before, 9, (east, far_day))
    west_direct = pair(low, after, 11, (west, far_day))
    east_relay = tuple(
        remote(far.at[last, part], far.at[before, part], 9 + i, (east, day)) for i, part in enumerate((head_rows, tail_rows))
    )
    west_relay = tuple(
        remote(far.at[first, part], far.at[after, part], 11 + i, (west, day)) for i, part in enumerate((head_rows, tail_rows))
    )
    bulk = [
        pair(pl.ds(edge + STEP * k, STEP), pl.ds(2 * edge + STEP * k, STEP), 13 + 2 * k, (here, far_day))
        for k in range(chunks)
    ]

    def start(copies):
        for copy in copies:
            copy.start()

    def arrive(copies):
        for copy in copies:
            copy.wait_recv()

    start((*far_edges, to_east, to_west))

    @pl.when(plane == PLANES - 1)
    def _():
        start(east_direct)

    @pl.when(plane == 0)
    def _():
        start(west_direct)

    near_all.start()
    for chunk in bulk:
        start(chunk)

    arrive((to_east, to_west))
    start((near_before, near_after))
    arrive(far_edges)

    @pl.when(plane != PLANES - 1)
    def _():
        start(east_relay)

    @pl.when(plane != 0)
    def _():
        start(west_relay)

    load.wait()
    near_all.wait_recv()

    def term(lon, _):
        total = jnp.dot(weights[core, 0], own[lon], preferred_element_type=jnp.float32)
        total += jnp.dot(weights[core, 1], near[lon], preferred_element_type=jnp.float32)
        total += jnp.dot(weights[core, 2, :, 0 : 2 * TILE], far[lon], preferred_element_type=jnp.float32)
        terms[lon] = total
        return _

    scale = 1.0 / ((2 * DAY_HALF + 1) * (2 * LON_HALF + 1))

    def result(lon, total):
        total = total + terms[lon + 2 * edge]
        done[lon] = total * scale
        return total - terms[lon]

    def put(start, size):
        return pltpu.make_async_copy(done.at[pl.ds(start, size)], out.at[pl.ds(start, size)], out_sem)

    arrive((near_before, near_after, *east_relay, *west_relay))
    lax.fori_loop(0, 2 * edge, term, 0)
    lax.fori_loop(count, wide, term, 0)
    total = lax.fori_loop(0, 2 * edge, lambda lon, total: total + terms[lon], jnp.zeros(terms.shape[1:], jnp.float32))
    for k in range(chunks):
        arrive(bulk[k])
        lax.fori_loop(2 * edge + STEP * k, 2 * edge + STEP * (k + 1), term, 0)
        total = lax.fori_loop(STEP * k, STEP * (k + 1), result, total)
        put(STEP * k, STEP).start()
    total = lax.fori_loop(STEP * chunks, count, result, total)
    put(STEP * chunks, count - STEP * chunks).start()

    sent = [to_east, to_west, *far_edges, near_all, near_before, near_after, *east_relay, *west_relay]
    for chunk in bulk:
        sent += chunk
    for copy in sent:
        copy.wait_send()
    put(0, count).wait()


def day_weights(rows):
    width = 2 * DAY_HALF + 1
    span = np.arange(-DAY_HALF, rows + DAY_HALF)
    window = np.abs(span[None, :] - np.arange(rows)[:, None]) <= DAY_HALF
    full = width * (span[None, :] == np.arange(rows)[:, None]) - 1.0 * window
    earlier, middle, later = full[:, :DAY_HALF], full[:, DAY_HALF : DAY_HALF + rows], full[:, DAY_HALF + rows :]
    table = np.zeros((2, 3, rows, rows), np.float32)
    table[:, 0] = middle
    table[0, 1, :, :DAY_HALF] = later
    table[1, 1, :, rows - DAY_HALF :] = earlier
    table[0, 2, :, :TILE] = earlier[:, :TILE]
    table[0, 2, :, TILE + 1 : 2 * TILE] = earlier[:, TILE:]
    table[1, 2, :, :DAY_HALF] = later
    return jnp.asarray(table, jnp.bfloat16)


def solution(mesh):
    lons, days = mesh.shape["lon"], mesh.shape["day"]

    def local(field):
        rows, count, columns = field.shape
        wide = count + 2 * LON_HALF
        slots = 13 + 2 * ((count - 2 * LON_HALF) // STEP)
        turned = jnp.transpose(field, (1, 0, 2))
        core = lax.rem(lax.axis_index("day"), 2)
        tail = jnp.where(core == 0, turned[:, TILE : 2 * TILE], turned[:, rows - TILE :])
        result = pl.pallas_call(
            functools.partial(kernel, lons, days),
            out_shape=jax.ShapeDtypeStruct((count, rows, columns), jnp.float32),
            in_specs=[pl.BlockSpec(memory_space=pl.ANY), pl.BlockSpec(memory_space=pl.ANY), pl.BlockSpec(memory_space=pltpu.VMEM)],
            out_specs=pl.BlockSpec(memory_space=pl.ANY),
            scratch_shapes=[
                pltpu.VMEM((wide, rows, columns), jnp.bfloat16),
                pltpu.VMEM((wide, rows, columns), jnp.bfloat16),
                pltpu.VMEM((wide, 2 * TILE, columns), jnp.bfloat16),
                pltpu.VMEM((wide, rows, columns), jnp.float32),
                pltpu.VMEM((count, rows, columns), jnp.float32),
                pltpu.SemaphoreType.DMA,
                pltpu.SemaphoreType.DMA((slots,)),
                pltpu.SemaphoreType.DMA((slots,)),
                pltpu.SemaphoreType.DMA,
            ],
            compiler_params=pltpu.CompilerParams(
                collective_id=0, has_side_effects=True, vmem_limit_bytes=60 * 1024 * 1024
            ),
            name="anomaly",
        )(turned, tail, day_weights(rows))
        return jnp.transpose(result, (1, 0, 2))

    return jax.shard_map(
        local, mesh=mesh, in_specs=(P("day", "lon", None),), out_specs=P("day", "lon", None), check_vma=False
    )
```

time: 158 us -> 102 us (0.65)
  Pallas kernels: 0 us -> 89.2 us
  waiting for transfers between devices: 81.6 us -> 0 us
  other arithmetic: 49.6 us -> 3.89 us
  starting transfers between devices: 11.6 us -> 0 us
  local copies, waits for them, and re-layouts: 14.4 us -> 8.84 us
    pallas_call x0 -> x1, Pallas kernels: none -> 89.2 us  [local(): pl.pallas_call(functools.partial(kernel, lons, days), out_shape=jax.Shape...]
    ppermute x4 -> x0, waiting for transfers between devices: 81.6 us -> none  [the longest x2 68.8 us: extended(): lax.ppermute(tail, axis, [(i, (i + 1) % count) for i in range(count)])]
    another operation x2 -> x0, other arithmetic: 19.4 us -> none  [running(): total = jnp.cumsum(values, axis=dim)]
    convert_element_type x1 -> x0, other arithmetic: 13.1 us -> none  [local(): values = tall.astype(jnp.float32)]
    ppermute x4 -> x0, starting transfers between devices: 11.6 us -> none  [the longest x2 8.6 us: extended(): lax.ppermute(head, axis, [((i + 1) % count, i) for i in range(count)])]
    sub x1 -> x0, other arithmetic: 7.71 us -> none  [local(): anomaly = values[DAY_HALF:values.shape[0] - DAY_HALF] - clim]
    concatenate x1 -> x0, other arithmetic: 4.81 us -> none  [extended(): jnp.concatenate([lax.ppermute(tail, axis, [(i, (i + 1) % count) for i in...]
    div x1 -> x0, other arithmetic: 4.63 us -> none  [running(): return (upper - lower) / (2.0 * half + 1.0)]
  transfers between devices with their start and end apart: 4 -> 0, of which waited for: 4 -> 0; matrix products, arithmetic and copies ran while one was open for 1% -> 0% of each run, Pallas kernels for 0% -> 0%
where the time goes in v1:
time: 102 us
  Pallas kernels  89.2 us (87%)
  local copies, waits for them, and re-layouts  8.84 us (9%)
  other arithmetic  3.89 us (4%)
    pallas_call x1, Pallas kernels, local(): pl.pallas_call(functools.partial(kernel, lons, days), out_shape=jax.Shape...  89.2 us
    unnamed x1, local copies, waits for them, and re-layouts  8.84 us
    select_n x1, other arithmetic, local(): jnp.where(core == 0, turned[:, TILE:2 * TILE], turned[:, rows - TILE:])  3.89 us

profile of v1, /device:TPU:1, one launch (start us, length us, event | category | flops | bytes accessed | tf_op | source)
XLA Modules:
  0.0 102.0 jit_solution(3515969840486308050)
XLA Ops:
  0.0 3.9 %slice_select_fusion.tail = bf16[90,8,1024]{2,1,0:T(8,128)(2,1)} fusion(bf16[90,23,1024]{2,1,0:T(8,128)(2,1)} %bitcast.3, pred[]{:T(512)S(6)} %eq.3), kind=kLoop, calls=%fused_computation | loop fusion | flops 737280 | bytes 4423681 | tf_op jit(solution)/shard_map/jit(_where)/select_n | solution.py:179
  3.9 89.2 %anomaly.1 = f32[90,23,1024]{2,1,0:T(8,128)} custom-call(bf16[90,23,1024]{2,1,0:T(8,128)(2,1)} %bitcast.4, bf16[90,8,1024]{2,1,0:T(8,128)(2,1)} %slice_select_fusion.tail, bf16[2,3,23,23]{3,2,1,0:T(8,128)(2,1)} %constant.12.clone.weights), custom_call_target="tpu_custom_call" | custom-call | tf_op jit(solution)/shard_map/anomaly/pallas_call | solution.py:180
  93.1 8.8 %copy.4 = f32[23,90,1024]{2,0,1:T(8,128)} copy(f32[23,90,1024]{2,0,1:T(8,128)} %bitcast.2) | data formatting | bytes 16957440

commit v2 on v1

v2 whole, which is shorter than its diff:
```python
import functools

import jax
import jax.numpy as jnp
import numpy as np
from jax import lax
from jax.experimental import pallas as pl
from jax.experimental.pallas import tpu as pltpu
from jax.sharding import PartitionSpec as P

DAY_HALF = 15
LON_HALF = 10
PLANES = 8
TILE = 8
REST = DAY_HALF - TILE
STEP = LON_HALF
PACKED = (STEP - 1) * TILE
MESH = pl.DeviceIdType.MESH


def kernel(lons, days, field, weights, out, own, near, heads, tails, packed, terms, local_sem, send, recv):
    count = field.shape[0]
    columns = field.shape[2]
    groups = count // STEP
    here = lax.axis_index("lon")
    day = lax.axis_index("day")
    core = lax.rem(day, 2)
    turn = 2 * core - 1
    far_day = lax.rem(day + turn + days, days)
    near_day = lax.rem(day - turn + days, days)
    east = lax.rem(here + 1, lons)
    west = lax.rem(here + lons - 1, lons)
    plane = lax.rem(here, PLANES)

    partners = ((here, far_day), (here, near_day), (east, day), (west, day), (east, far_day), (west, far_day))
    barrier = pltpu.get_barrier_semaphore()
    for partner in partners:
        pl.semaphore_signal(barrier, inc=1, device_id=partner, device_id_type=MESH)
    load = pltpu.make_async_copy(field, own.at[pl.ds(STEP, count)], local_sem)
    load.start()
    pl.semaphore_wait(barrier, len(partners))

    def remote(source, target, slot, device):
        return pltpu.make_async_remote_copy(
            src_ref=source, dst_ref=target, send_sem=send.at[slot], recv_sem=recv.at[slot],
            device_id=device, device_id_type=MESH,
        )

    def start(*copies):
        for copy in copies:
            copy.start()

    def arrive(*copies):
        for copy in copies:
            copy.wait_recv()

    def span(group):
        return pl.ds(STEP * group, STEP)

    head_rows = pl.ds(pl.multiple_of(TILE * core, TILE), TILE)
    final = groups - 1

    to_east = remote(field.at[span(final)], own.at[span(0)], 0, (east, day))
    to_west = remote(field.at[span(0)], own.at[span(groups + 1)], 1, (west, day))
    near_all = remote(field, near.at[pl.ds(STEP, count)], 2, (here, near_day))
    near_west = remote(own.at[span(0)], near.at[span(0)], 3, (here, near_day))
    near_east = remote(own.at[span(groups + 1)], near.at[span(groups + 1)], 4, (here, near_day))
    east_head_direct = remote(field.at[span(final), head_rows], heads.at[span(0)], 5, (east, far_day))
    west_head_direct = remote(field.at[span(0), head_rows], heads.at[span(groups + 1)], 6, (west, far_day))
    east_tail_direct = remote(packed.at[final], tails.at[0], 7, (east, far_day))
    west_tail_direct = remote(packed.at[0], tails.at[groups + 1], 8, (west, far_day))
    east_head = remote(heads.at[span(groups)], heads.at[span(0)], 5, (east, day))
    west_head = remote(heads.at[span(1)], heads.at[span(groups + 1)], 6, (west, day))
    east_tail = remote(tails.at[groups], tails.at[0], 7, (east, day))
    west_tail = remote(tails.at[1], tails.at[groups + 1], 8, (west, day))
    far_head = [
        remote(field.at[span(g), head_rows], heads.at[span(g + 1)], 9 + g, (here, far_day)) for g in range(groups)
    ]
    far_tail = [remote(packed.at[g], tails.at[g + 1], 9 + groups + g, (here, far_day)) for g in range(groups)]

    start(far_head[0], far_head[final], to_east, to_west)

    @pl.when(plane == PLANES - 1)
    def _():
        start(east_head_direct)

    @pl.when(plane == 0)
    def _():
        start(west_head_direct)

    start(near_all)
    load.wait()

    def rest(lon):
        rows = pl.ds(pl.multiple_of(TILE + TILE * core, TILE), REST)
        return own[lon, rows, :].astype(jnp.float32)

    def pack(group, _):
        base = STEP * (group + 1)
        spare = rest(base + STEP - 1)
        for j in range(STEP - 1):
            extra = spare[j % REST : j % REST + 1]
            tile = jnp.concatenate([rest(base + j), extra], axis=0)
            packed[group, TILE * j : TILE * (j + 1), :] = tile.astype(jnp.bfloat16)
        return _

    lax.fori_loop(0, groups, pack, 0)

    arrive(to_east, to_west)
    start(near_west, near_east, far_tail[0], far_tail[final])

    @pl.when(plane == PLANES - 1)
    def _():
        start(east_tail_direct)

    @pl.when(plane == 0)
    def _():
        start(west_tail_direct)

    for g in range(1, final):
        start(far_head[g], far_tail[g])

    arrive(far_head[0], far_head[final], far_tail[0], far_tail[final])

    @pl.when(plane != PLANES - 1)
    def _():
        start(east_head, east_tail)

    @pl.when(plane != 0)
    def _():
        start(west_head, west_tail)

    def term(group, _):
        base = STEP * group
        for j in range(STEP):
            lon = base + j
            total = jnp.dot(weights[core, 0, :, 0 : own.shape[1]], own[lon], preferred_element_type=jnp.float32)
            total += jnp.dot(weights[core, 1, :, 0 : own.shape[1]], near[lon], preferred_element_type=jnp.float32)
            total += jnp.dot(weights[core, 2, :, 0:TILE], heads[lon], preferred_element_type=jnp.float32)
            if j < STEP - 1:
                tile = tails[group, TILE * j : TILE * (j + 1), :]
                total += jnp.dot(weights[core, 3, :, 0:TILE], tile, preferred_element_type=jnp.float32)
            else:
                total += jnp.dot(weights[core, 4], tails[group], preferred_element_type=jnp.float32)
            terms[lon] = total
        return _

    scale = 1.0 / ((2 * DAY_HALF + 1) * (2 * LON_HALF + 1))

    def result(lon, total):
        total = total + terms[lon + 2 * STEP]
        out[lon] = total * scale
        return total - terms[lon]

    def results(group, total):
        return lax.fori_loop(STEP * group, STEP * (group + 1), result, total)

    def opening(group):
        zero = jnp.zeros(terms.shape[1:], jnp.float32)
        return lax.fori_loop(STEP * group, STEP * (group + 2), lambda lon, total: total + terms[lon], zero)

    arrive(near_all)
    lax.fori_loop(0, 2, lambda i, c: term(1 + final * i, c), 0)
    arrive(far_head[1], far_tail[1])
    term(2, 0)
    total = opening(1)
    corner = final // 2 + 1
    for g in range(2, final):
        arrive(far_head[g], far_tail[g])
        term(g + 1, 0)
        total = results(g - 1, total)
        if g == corner:
            arrive(near_west, near_east, east_head, west_head, east_tail, west_tail)
            lax.fori_loop(0, 2, lambda i, c: term((groups + 1) * i, c), 0)
            results(0, opening(0))
    for g in range(final - 1, groups):
        total = results(g, total)

    for copy in (to_east, to_west, near_all, near_west, near_east, east_head, west_head, east_tail, west_tail):
        copy.wait_send()
    for copy in far_head + far_tail:
        copy.wait_send()


def day_weights(rows):
    width = 2 * DAY_HALF + 1
    span = np.arange(-DAY_HALF, rows + DAY_HALF)
    window = np.abs(span[None, :] - np.arange(rows)[:, None]) <= DAY_HALF
    full = width * (span[None, :] == np.arange(rows)[:, None]) - 1.0 * window
    earlier, middle, later = full[:, :DAY_HALF], full[:, DAY_HALF : DAY_HALF + rows], full[:, DAY_HALF + rows :]
    table = np.zeros((2, 5, rows, PACKED), np.float32)
    table[:, 0, :, :rows] = middle
    table[0, 1, :, :DAY_HALF] = later
    table[1, 1, :, rows - DAY_HALF : rows] = earlier
    for core, far in enumerate((earlier, later)):
        table[core, 2, :, :TILE] = far[:, :TILE]
        table[core, 3, :, :REST] = far[:, TILE:]
        for j in range(REST):
            table[core, 4, :, TILE * j + REST] = far[:, TILE + j]
    return jnp.asarray(table, jnp.bfloat16)


def solution(mesh):
    lons, days = mesh.shape["lon"], mesh.shape["day"]

    def local(field):
        rows, count, columns = field.shape
        groups = count // STEP
        wide = count + 2 * STEP
        slots = 9 + 2 * groups
        result = pl.pallas_call(
            functools.partial(kernel, lons, days),
            out_shape=pltpu.VMEM((count, rows, columns), jnp.float32),
            in_specs=[pl.BlockSpec(memory_space=pltpu.HBM), pl.BlockSpec(memory_space=pltpu.VMEM)],
            out_specs=pl.BlockSpec(memory_space=pltpu.VMEM),
            scratch_shapes=[
                pltpu.VMEM((wide, rows, columns), jnp.bfloat16),
                pltpu.VMEM((wide, rows, columns), jnp.bfloat16),
                pltpu.VMEM((wide, TILE, columns), jnp.bfloat16),
                pltpu.VMEM((groups + 2, PACKED, columns), jnp.bfloat16),
                pltpu.VMEM((groups, PACKED, columns), jnp.bfloat16),
                pltpu.VMEM((wide, rows, columns), jnp.float32),
                pltpu.SemaphoreType.DMA,
                pltpu.SemaphoreType.DMA((slots,)),
                pltpu.SemaphoreType.DMA((slots,)),
            ],
            compiler_params=pltpu.CompilerParams(
                collective_id=0, has_side_effects=True, vmem_limit_bytes=44 * 1024 * 1024
            ),
            name="anomaly",
        )(jnp.transpose(field, (1, 0, 2)), day_weights(rows))
        return jnp.transpose(result, (1, 0, 2))

    return jax.shard_map(
        local, mesh=mesh, in_specs=(P("day", "lon", None),), out_specs=P("day", "lon", None), check_vma=False
    )
```

time: 102 us -> 88.5 us (0.87)
  Pallas kernels: 89.2 us -> 84 us
  local copies, waits for them, and re-layouts: 8.84 us -> 4.38 us
  other arithmetic: 3.89 us -> 0 us
    pallas_call x1, Pallas kernels: 89.2 us -> 84 us  [local(): pl.pallas_call(functools.partial(kernel, lons, days), out_shape=pltpu.VME...]
    unnamed x1 -> x3, local copies, waits for them, and re-layouts: 8.84 us -> 4.38 us
    select_n x1 -> x0, other arithmetic: 3.89 us -> none  [local(): jnp.where(core == 0, turned[:, TILE:2 * TILE], turned[:, rows - TILE:])]
where the time goes in v2:
time: 88.5 us; the launch traced here: 88.4 us
  Pallas kernels  84 us (95%)
  local copies, waits for them, and re-layouts  4.38 us (5%)
    pallas_call x1, Pallas kernels, local(): pl.pallas_call(functools.partial(kernel, lons, days), out_shape=pltpu.VME...  84 us
    unnamed x3, local copies, waits for them, and re-layouts  4.38 us

profile of v2, /device:TPU:1, one launch (start us, length us, event | category | flops | bytes accessed | tf_op | source)
XLA Modules:
  0.0 88.4 jit_solution(10148189788367309499)
XLA Ops:
  0.0 0.0 copy-start
  0.0 0.8 copy-done
  0.8 84.0 %anomaly.1 = f32[90,23,1024]{2,1,0:T(8,128)S(1)} custom-call(bf16[90,23,1024]{2,1,0:T(8,128)(2,1)} %bitcast.3, bf16[2,5,23,72]{3,2,1,0:T(8,128)(2,1)S(1)} %copy-done), custom_call_target="tpu_custom_call" | custom-call | tf_op jit(solution)/shard_map/anomaly/pallas_call | solution.py:211
  84.8 3.6 %copy.4 = f32[23,90,1024]{2,0,1:T(8,128)} copy(f32[23,90,1024]{2,0,1:T(8,128)S(1)} %bitcast.2) | data formatting | bytes 16957440
Async XLA Ops:
  0.0 0.8 copy-start

commit v3 on v2

--- a/solution.py
+++ b/solution.py
@@ -2,7 +2,6 @@
 
 import jax
 import jax.numpy as jnp
-import numpy as np
 from jax import lax
 from jax.experimental import pallas as pl
 from jax.experimental.pallas import tpu as pltpu
@@ -15,10 +14,13 @@
 REST = DAY_HALF - TILE
 STEP = LON_HALF
 PACKED = (STEP - 1) * TILE
+RELAYS = 3
+SHARE = 3
+KEPT = STEP - RELAYS * SHARE
 MESH = pl.DeviceIdType.MESH
 
 
-def kernel(lons, days, field, weights, out, own, near, heads, tails, packed, terms, local_sem, send, recv):
+def kernel(lons, days, field, out, own, near, heads, tails, packed, terms, weights, relayed, ready, local_sem, send, recv):
     count = field.shape[0]
     columns = field.shape[2]
     groups = count // STEP
@@ -32,17 +34,56 @@
     west = lax.rem(here + lons - 1, lons)
     plane = lax.rem(here, PLANES)
 
-    partners = ((here, far_day), (here, near_day), (east, day), (west, day), (east, far_day), (west, far_day))
     barrier = pltpu.get_barrier_semaphore()
-    for partner in partners:
-        pl.semaphore_signal(barrier, inc=1, device_id=partner, device_id_type=MESH)
+
+    def level(offset):
+        return lax.rem(here + offset + lons, lons)
+
+    def greet(*partners):
+        for partner in partners:
+            pl.semaphore_signal(barrier, inc=1, device_id=partner, device_id_type=MESH)
+
+    reach = range(1, RELAYS + 1)
+    eastmost = plane == PLANES - 1
+
+    def at(spot):
+        return functools.partial(pl.when, plane == spot)
+
+    greet((here, far_day), (here, near_day))
+    pl.when(plane != PLANES - 1)(functools.partial(greet, (east, day)))
+    at(0)()(
+        functools.partial(
+            greet, (west, day), (west, far_day), *[(level(k), day) for k in reach[1:]], *[(level(-k - 1), day) for k in reach]
+        )
+    )
+    for k in reach:
+        at(k)()(functools.partial(greet, (level(-k - 1), day)))
+    for k in reach[1:]:
+        at(PLANES - 1 - k)()(functools.partial(greet, (level(k), day)))
     load = pltpu.make_async_copy(field, own.at[pl.ds(STEP, count)], local_sem)
     load.start()
-    pl.semaphore_wait(barrier, len(partners))
-
-    def remote(source, target, slot, device):
+    waits = {0: 2, 1: 3, PLANES - 1: 4 + 2 * RELAYS}
+    for spot in range(PLANES):
+        at(spot)()(functools.partial(pl.semaphore_wait, barrier, waits.get(spot, 4)))
+
+    def tell(slot, *partners):
+        for partner in partners:
+            pl.semaphore_signal(ready.at[slot], inc=1, device_id=partner, device_id_type=MESH)
+
+    pl.when(plane != 0)(functools.partial(tell, 0, (west, day)))
+
+    @pl.when(eastmost)
+    def _():
+        tell(1, (east, day))
+        tell(2, (east, far_day))
+        tell(3, *[(level(-k), day) for k in reach[1:]])
+
+    for k in reach:
+        at(PLANES - 1 - k)()(functools.partial(tell, 4, (level(k + 1), day)))
+
+    def remote(source, target, slot, device, sent=None):
         return pltpu.make_async_remote_copy(
-            src_ref=source, dst_ref=target, send_sem=send.at[slot], recv_sem=recv.at[slot],
+            src_ref=source, dst_ref=target, send_sem=send.at[slot if sent is None else sent], recv_sem=recv.at[slot],
             device_id=device, device_id_type=MESH,
         )
 
@@ -73,20 +114,40 @@
     west_head = remote(heads.at[span(1)], heads.at[span(groups + 1)], 6, (west, day))
     east_tail = remote(tails.at[groups], tails.at[0], 7, (east, day))
     west_tail = remote(tails.at[1], tails.at[groups + 1], 8, (west, day))
+    spot = 9 + 2 * groups
+    cut = [pl.ds(KEPT + SHARE * (k - 1), SHARE) for k in reach]
+    east_part = [remote(field.at[pl.ds(STEP * final, KEPT)], own.at[pl.ds(0, KEPT)], 0, (east, day))]
+    east_part += [
+        remote(field.at[pl.ds(STEP * final + cut[k - 1].start, SHARE)], relayed, spot, (level(k + 1), day), spot + k)
+        for k in reach
+    ]
+    west_part = [remote(field.at[pl.ds(0, KEPT)], own.at[pl.ds(STEP * (groups + 1), KEPT)], 1, (west, day))]
+    west_part += [remote(field.at[cut[k - 1]], relayed, spot, (level(-k - 1), day), spot + k) for k in reach]
+    east_pass = [remote(relayed, own.at[cut[k - 1]], 0, (level(-k), day), spot) for k in reach]
+    west_pass = [
+        remote(relayed, own.at[pl.ds(STEP * (groups + 1) + cut[k - 1].start, SHARE)], 1, (level(k), day), spot)
+        for k in reach
+    ]
+
+    def each_plane(eastward, westward, act):
+        for k in reach:
+            pl.when(plane == k)(functools.partial(act, eastward[k - 1]))
+            pl.when(plane == PLANES - 1 - k)(functools.partial(act, westward[k - 1]))
+
     far_head = [
         remote(field.at[span(g), head_rows], heads.at[span(g + 1)], 9 + g, (here, far_day)) for g in range(groups)
     ]
     far_tail = [remote(packed.at[g], tails.at[g + 1], 9 + groups + g, (here, far_day)) for g in range(groups)]
 
-    start(far_head[0], far_head[final], to_east, to_west)
-
-    @pl.when(plane == PLANES - 1)
-    def _():
-        start(east_head_direct)
-
-    @pl.when(plane == 0)
-    def _():
-        start(west_head_direct)
+    start(far_head[0], far_head[final])
+
+    @pl.when(eastmost)
+    def _():
+        start(*reversed(east_part), east_head_direct)
+
+    @pl.when(plane != 0)
+    def _():
+        start(to_west)
 
     start(near_all)
     load.wait()
@@ -106,20 +167,36 @@
 
     lax.fori_loop(0, groups, pack, 0)
 
-    arrive(to_east, to_west)
-    start(near_west, near_east, far_tail[0], far_tail[final])
-
-    @pl.when(plane == PLANES - 1)
+    start(far_tail[0], far_tail[final])
+
+    @pl.when(eastmost)
     def _():
         start(east_tail_direct)
-
-    @pl.when(plane == 0)
-    def _():
-        start(west_tail_direct)
 
     for g in range(1, final):
         start(far_head[g], far_tail[g])
 
+    @pl.when(plane != PLANES - 1)
+    def _():
+        pl.semaphore_wait(ready.at[0], 1)
+        start(to_east)
+
+    @pl.when(plane == 0)
+    def _():
+        for slot, count_of in ((1, 1), (2, 1), (4, RELAYS)):
+            pl.semaphore_wait(ready.at[slot], count_of)
+        start(*reversed(west_part), west_head_direct, west_tail_direct)
+
+    for k in reach[1:]:
+        at(PLANES - 1 - k)()(functools.partial(pl.semaphore_wait, ready.at[3], 1))
+
+    def forward(copy):
+        arrive(east_part[1])
+        start(copy)
+
+    each_plane(east_pass, west_pass, forward)
+    arrive(to_east, to_west)
+    start(near_west, near_east)
     arrive(far_head[0], far_head[final], far_tail[0], far_tail[final])
 
     @pl.when(plane != PLANES - 1)
@@ -129,19 +206,36 @@
     @pl.when(plane != 0)
     def _():
         start(west_head, west_tail)
+
+    day_of = lax.broadcasted_iota(jnp.int32, weights.shape[1:], 0)
+    place = lax.broadcasted_iota(jnp.int32, weights.shape[1:], 1)
+
+    def window(position, valid=True):
+        inside = (jnp.abs(position - day_of) <= DAY_HALF) & valid
+        return jnp.where(inside, -1.0, 0.0)
+
+    block = own.shape[1]
+    earlier, later = 1 - core, core
+    weights[0] = (window(place) + jnp.where(place == day_of, 2.0 * DAY_HALF + 1.0, 0.0)).astype(jnp.bfloat16)
+    weights[1] = window(place + block * (earlier - later)).astype(jnp.bfloat16)
+    weights[2] = window(place - DAY_HALF * earlier + block * later).astype(jnp.bfloat16)
+    weights[3] = window(place - REST * earlier + (block + TILE) * later, place < REST).astype(jnp.bfloat16)
+    which = place // TILE
+    stray = (place % TILE == REST) & (which < REST)
+    weights[4] = window(which - REST * earlier + (block + TILE) * later, stray).astype(jnp.bfloat16)
 
     def term(group, _):
         base = STEP * group
         for j in range(STEP):
             lon = base + j
-            total = jnp.dot(weights[core, 0, :, 0 : own.shape[1]], own[lon], preferred_element_type=jnp.float32)
-            total += jnp.dot(weights[core, 1, :, 0 : own.shape[1]], near[lon], preferred_element_type=jnp.float32)
-            total += jnp.dot(weights[core, 2, :, 0:TILE], heads[lon], preferred_element_type=jnp.float32)
+            total = jnp.dot(weights[0, :, 0 : own.shape[1]], own[lon], preferred_element_type=jnp.float32)
+            total += jnp.dot(weights[1, :, 0 : own.shape[1]], near[lon], preferred_element_type=jnp.float32)
+            total += jnp.dot(weights[2, :, 0:TILE], heads[lon], preferred_element_type=jnp.float32)
             if j < STEP - 1:
                 tile = tails[group, TILE * j : TILE * (j + 1), :]
-                total += jnp.dot(weights[core, 3, :, 0:TILE], tile, preferred_element_type=jnp.float32)
+                total += jnp.dot(weights[3, :, 0:TILE], tile, preferred_element_type=jnp.float32)
             else:
-                total += jnp.dot(weights[core, 4], tails[group], preferred_element_type=jnp.float32)
+                total += jnp.dot(weights[4], tails[group], preferred_element_type=jnp.float32)
             terms[lon] = total
         return _
 
@@ -176,28 +270,32 @@
     for g in range(final - 1, groups):
         total = results(g, total)
 
-    for copy in (to_east, to_west, near_all, near_west, near_east, east_head, west_head, east_tail, west_tail):
+    def finish(*copies):
+        for copy in copies:
+            copy.wait_send()
+
+    each_plane(east_pass, west_pass, finish)
+
+    @pl.when(plane == PLANES - 1)
+    def _():
+        finish(*east_part)
+
+    @pl.when(plane != PLANES - 1)
+    def _():
+        finish(to_east)
+
+    @pl.when(plane == 0)
+    def _():
+        finish(*west_part)
+
+    @pl.when(plane != 0)
+    def _():
+        finish(to_west)
+
+    for copy in (near_all, near_west, near_east, east_head, west_head, east_tail, west_tail):
         copy.wait_send()
     for copy in far_head + far_tail:
         copy.wait_send()
-
-
-def day_weights(rows):
-    width = 2 * DAY_HALF + 1
-    span = np.arange(-DAY_HALF, rows + DAY_HALF)
-    window = np.abs(span[None, :] - np.arange(rows)[:, None]) <= DAY_HALF
-    full = width * (span[None, :] == np.arange(rows)[:, None]) - 1.0 * window
-    earlier, middle, later = full[:, :DAY_HALF], full[:, DAY_HALF : DAY_HALF + rows], full[:, DAY_HALF + rows :]
-    table = np.zeros((2, 5, rows, PACKED), np.float32)
-    table[:, 0, :, :rows] = middle
-    table[0, 1, :, :DAY_HALF] = later
-    table[1, 1, :, rows - DAY_HALF : rows] = earlier
-    for core, far in enumerate((earlier, later)):
-        table[core, 2, :, :TILE] = far[:, :TILE]
-        table[core, 3, :, :REST] = far[:, TILE:]
-        for j in range(REST):
-            table[core, 4, :, TILE * j + REST] = far[:, TILE + j]
-    return jnp.asarray(table, jnp.bfloat16)
 
 
 def solution(mesh):
@@ -207,11 +305,11 @@
         rows, count, columns = field.shape
         groups = count // STEP
         wide = count + 2 * STEP
-        slots = 9 + 2 * groups
+        slots = 10 + 2 * groups + RELAYS
         result = pl.pallas_call(
             functools.partial(kernel, lons, days),
             out_shape=pltpu.VMEM((count, rows, columns), jnp.float32),
-            in_specs=[pl.BlockSpec(memory_space=pltpu.HBM), pl.BlockSpec(memory_space=pltpu.VMEM)],
+            in_specs=[pl.BlockSpec(memory_space=pltpu.HBM)],
             out_specs=pl.BlockSpec(memory_space=pltpu.VMEM),
             scratch_shapes=[
                 pltpu.VMEM((wide, rows, columns), jnp.bfloat16),
@@ -220,6 +318,9 @@
                 pltpu.VMEM((groups + 2, PACKED, columns), jnp.bfloat16),
                 pltpu.VMEM((groups, PACKED, columns), jnp.bfloat16),
                 pltpu.VMEM((wide, rows, columns), jnp.float32),
+                pltpu.VMEM((5, rows, PACKED), jnp.bfloat16),
+                pltpu.VMEM((SHARE, rows, columns), jnp.bfloat16),
+                pltpu.SemaphoreType.REGULAR((5,)),
                 pltpu.SemaphoreType.DMA,
                 pltpu.SemaphoreType.DMA((slots,)),
                 pltpu.SemaphoreType.DMA((slots,)),
@@ -228,7 +329,7 @@
                 collective_id=0, has_side_effects=True, vmem_limit_bytes=44 * 1024 * 1024
             ),
             name="anomaly",
-        )(jnp.transpose(field, (1, 0, 2)), day_weights(rows))
+        )(jnp.transpose(field, (1, 0, 2)))
         return jnp.transpose(result, (1, 0, 2))
 
     return jax.shard_map(

time: 88.5 us -> 73.3 us (0.83)
  the two profiles are of different devices: /device:TPU:1 before, /device:TPU:225 now
where the time goes in v3:
time: 73.3 us; the launch traced here: 73.2 us
  Pallas kernels  69.6 us (95%)
  local copies, waits for them, and re-layouts  3.55 us (5%)
    pallas_call x1, Pallas kernels, local(): pl.pallas_call(functools.partial(kernel, lons, days), out_shape=pltpu.VME...  69.6 us
    unnamed x1, local copies, waits for them, and re-layouts  3.55 us

profile of v3, /device:TPU:225, one launch (start us, length us, event | category | flops | bytes accessed | tf_op | source)
XLA Modules:
  0.0 73.2 jit_solution(5075101718024360030)
XLA Ops:
  0.0 69.6 %anomaly.1 = f32[90,23,1024]{2,1,0:T(8,128)S(1)} custom-call(bf16[90,23,1024]{2,1,0:T(8,128)(2,1)} %bitcast.3), custom_call_target="tpu_custom_call" | custom-call | tf_op jit(solution)/shard_map/anomaly/pallas_call | solution.py:309
  69.6 3.6 %copy.3 = f32[23,90,1024]{2,0,1:T(8,128)} copy(f32[23,90,1024]{2,0,1:T(8,128)S(1)} %bitcast.2) | data formatting | bytes 16957440

commit v4 on v3

--- a/solution.py
+++ b/solution.py
@@ -15,12 +15,52 @@
 STEP = LON_HALF
 PACKED = (STEP - 1) * TILE
 RELAYS = 3
+LATE = 3
 SHARE = 3
 KEPT = STEP - RELAYS * SHARE
 MESH = pl.DeviceIdType.MESH
 
 
-def kernel(lons, days, field, out, own, near, heads, tails, packed, terms, weights, relayed, ready, local_sem, send, recv):
+def results(terms, target, group, first, total):
+    scale = 1.0 / ((2 * DAY_HALF + 1) * (2 * LON_HALF + 1))
+
+    def result(lon, total):
+        total = total + terms[lon + 2 * STEP]
+        target[lon - STEP * first] = total * scale
+        return total - terms[lon]
+
+    return lax.fori_loop(STEP * group, STEP * (group + 1), result, total)
+
+
+def opening(terms, group):
+    zero = jnp.zeros(terms.shape[1:], jnp.float32)
+    return lax.fori_loop(STEP * group, STEP * (group + 2), lambda lon, total: total + terms[lon], zero)
+
+
+def finishing(done, terms, out, late, sems):
+    early = done.shape[0] // STEP
+
+    def put(source, group, first):
+        return pltpu.make_async_copy(
+            source.at[pl.ds(STEP * (group - first), STEP)], out.at[pl.ds(STEP * group, STEP)], sems.at[group]
+        )
+
+    copies = [put(done, group, 0) for group in range(early)]
+    for copy in copies:
+        copy.start()
+    total = opening(terms, early)
+    for group in range(early, early + LATE):
+        total = results(terms, late, group, early, total)
+        copies.append(put(late, group, early))
+        copies[-1].start()
+    for copy in copies:
+        copy.wait()
+
+
+def kernel(
+    lons, days, field, done, terms, own, near, heads, tails, packed, weights, relayed, ready,
+    apart, wrap_heads, wrap_tails, wrap_rests, side_heads, side_tails, side_rests, local_sem, send, recv,
+):
     count = field.shape[0]
     columns = field.shape[2]
     groups = count // STEP
@@ -116,18 +156,28 @@
     west_tail = remote(tails.at[1], tails.at[groups + 1], 8, (west, day))
     spot = 9 + 2 * groups
     cut = [pl.ds(KEPT + SHARE * (k - 1), SHARE) for k in reach]
-    east_part = [remote(field.at[pl.ds(STEP * final, KEPT)], own.at[pl.ds(0, KEPT)], 0, (east, day))]
-    east_part += [
-        remote(field.at[pl.ds(STEP * final + cut[k - 1].start, SHARE)], relayed, spot, (level(k + 1), day), spot + k)
-        for k in reach
-    ]
-    west_part = [remote(field.at[pl.ds(0, KEPT)], own.at[pl.ds(STEP * (groups + 1), KEPT)], 1, (west, day))]
-    west_part += [remote(field.at[cut[k - 1]], relayed, spot, (level(-k - 1), day), spot + k) for k in reach]
-    east_pass = [remote(relayed, own.at[cut[k - 1]], 0, (level(-k), day), spot) for k in reach]
-    west_pass = [
-        remote(relayed, own.at[pl.ds(STEP * (groups + 1) + cut[k - 1].start, SHARE)], 1, (level(k), day), spot)
-        for k in reach
-    ]
+    kept = pl.ds(0, KEPT)
+
+    turned = spot + RELAYS + 1
+    east_part = [remote(apart.at[kept], wrap_rests.at[kept], turned, (east, day))]
+    east_part += [remote(apart.at[cut[k - 1]], relayed, spot, (level(k + 1), day), spot + k) for k in reach]
+    west_part = [remote(apart.at[kept], wrap_rests.at[kept], turned, (west, day))]
+    west_part += [remote(apart.at[cut[k - 1]], relayed, spot, (level(-k - 1), day), spot + k) for k in reach]
+    east_pass = [remote(relayed, wrap_rests.at[cut[k - 1]], turned, (level(-k), day), spot) for k in reach]
+    west_pass = [remote(relayed, wrap_rests.at[cut[k - 1]], turned, (level(k), day), spot) for k in reach]
+    wrap_rest = remote(apart, wrap_rests, turned, (east, day))
+    east_wrap = (
+        remote(heads.at[span(groups)], wrap_heads, turned + 1, (east, far_day)),
+        remote(tails.at[groups], wrap_tails, turned + 2, (east, far_day)),
+    )
+    west_wrap = (
+        remote(heads.at[span(1)], wrap_heads, turned + 1, (west, far_day)),
+        remote(tails.at[1], wrap_tails, turned + 2, (west, far_day)),
+    )
+    sides = tuple(
+        remote(source, target, turned + 3 + i, (here, near_day))
+        for i, (source, target) in enumerate(((wrap_heads, side_heads), (wrap_tails, side_tails), (wrap_rests, side_rests)))
+    )
 
     def each_plane(eastward, westward, act):
         for k in reach:
@@ -143,7 +193,7 @@
 
     @pl.when(eastmost)
     def _():
-        start(*reversed(east_part), east_head_direct)
+        start(east_head_direct)
 
     @pl.when(plane != 0)
     def _():
@@ -167,11 +217,25 @@
 
     lax.fori_loop(0, groups, pack, 0)
 
+    ends = (plane == 0) | eastmost
+    wrapped = plane // (PLANES - 1)
+
+    @pl.when(ends)
+    def _():
+        def part(j, _):
+            lon = STEP + STEP * final * wrapped + j
+            low = own[lon, 0:TILE, :].astype(jnp.float32)
+            high = own[lon, TILE:, :].astype(jnp.float32)
+            apart[j] = jnp.where(core == 0, high[REST:], low).astype(jnp.bfloat16)
+            return _
+
+        lax.fori_loop(0, STEP, part, 0)
+
     start(far_tail[0], far_tail[final])
 
     @pl.when(eastmost)
     def _():
-        start(east_tail_direct)
+        start(*east_part, east_tail_direct)
 
     for g in range(1, final):
         start(far_head[g], far_tail[g])
@@ -185,7 +249,7 @@
     def _():
         for slot, count_of in ((1, 1), (2, 1), (4, RELAYS)):
             pl.semaphore_wait(ready.at[slot], count_of)
-        start(*reversed(west_part), west_head_direct, west_tail_direct)
+        start(*west_part, west_head_direct, west_tail_direct)
 
     for k in reach[1:]:
         at(PLANES - 1 - k)()(functools.partial(pl.semaphore_wait, ready.at[3], 1))
@@ -195,8 +259,17 @@
         start(copy)
 
     each_plane(east_pass, west_pass, forward)
-    arrive(to_east, to_west)
-    start(near_west, near_east)
+
+    @pl.when(plane != 0)
+    def _():
+        arrive(to_east)
+        start(near_west)
+
+    @pl.when(plane != PLANES - 1)
+    def _():
+        arrive(to_west)
+        start(near_east)
+
     arrive(far_head[0], far_head[final], far_tail[0], far_tail[final])
 
     @pl.when(plane != PLANES - 1)
@@ -206,6 +279,19 @@
     @pl.when(plane != 0)
     def _():
         start(west_head, west_tail)
+
+    @pl.when(eastmost)
+    def _():
+        start(*east_wrap)
+
+    @pl.when(plane == 0)
+    def _():
+        start(*west_wrap)
+
+    @pl.when(ends)
+    def _():
+        arrive(wrap_rest, *east_wrap)
+        start(*sides)
 
     day_of = lax.broadcasted_iota(jnp.int32, weights.shape[1:], 0)
     place = lax.broadcasted_iota(jnp.int32, weights.shape[1:], 1)
@@ -224,51 +310,71 @@
     stray = (place % TILE == REST) & (which < REST)
     weights[4] = window(which - REST * earlier + (block + TILE) * later, stray).astype(jnp.bfloat16)
 
+    @pl.when(ends)
+    def _():
+        for i, (shift, which_core, center) in enumerate(((0, core, 1.0), (block * (earlier - later), 1 - core, 0.0))):
+            base = TILE + TILE * which_core + shift
+            spots = (
+                (place + base - TILE, True), (place + base, place < REST), (which + base, stray),
+                (place + DAY_HALF * (1 - which_core) + shift, True),
+            )
+            for n, (position, valid) in enumerate(spots):
+                peak = jnp.where((position == day_of) & valid, center * (2.0 * DAY_HALF + 1.0), 0.0)
+                weights[5 + 4 * i + n] = (window(position, valid) + peak).astype(jnp.bfloat16)
+
+    def dot(which, columns, values):
+        return jnp.dot(weights[which, :, 0:columns], values, preferred_element_type=jnp.float32)
+
+    def strip(first, tail, j):
+        if j < STEP - 1:
+            return dot(first, TILE, tail[TILE * j : TILE * (j + 1), :])
+        return dot(first + 1, PACKED, tail[...])
+
     def term(group, _):
-        base = STEP * group
         for j in range(STEP):
-            lon = base + j
-            total = jnp.dot(weights[0, :, 0 : own.shape[1]], own[lon], preferred_element_type=jnp.float32)
-            total += jnp.dot(weights[1, :, 0 : own.shape[1]], near[lon], preferred_element_type=jnp.float32)
-            total += jnp.dot(weights[2, :, 0:TILE], heads[lon], preferred_element_type=jnp.float32)
-            if j < STEP - 1:
-                tile = tails[group, TILE * j : TILE * (j + 1), :]
-                total += jnp.dot(weights[3, :, 0:TILE], tile, preferred_element_type=jnp.float32)
-            else:
-                total += jnp.dot(weights[4], tails[group], preferred_element_type=jnp.float32)
+            lon = STEP * group + j
+            total = dot(0, block, own[lon]) + dot(1, block, near[lon])
+            terms[lon] = total + dot(2, TILE, heads[lon]) + strip(3, tails.at[group], j)
+        return _
+
+    def wrap_term(group):
+        for j in range(STEP):
+            lon = STEP * group + j
+            total = dot(2, TILE, heads[lon]) + strip(3, tails.at[group], j)
+            total += dot(5, TILE, wrap_heads[j]) + strip(6, wrap_tails, j) + dot(8, TILE, wrap_rests[j])
+            total += dot(9, TILE, side_heads[j]) + strip(10, side_tails, j) + dot(12, TILE, side_rests[j])
             terms[lon] = total
-        return _
-
-    scale = 1.0 / ((2 * DAY_HALF + 1) * (2 * LON_HALF + 1))
-
-    def result(lon, total):
-        total = total + terms[lon + 2 * STEP]
-        out[lon] = total * scale
-        return total - terms[lon]
-
-    def results(group, total):
-        return lax.fori_loop(STEP * group, STEP * (group + 1), result, total)
-
-    def opening(group):
-        zero = jnp.zeros(terms.shape[1:], jnp.float32)
-        return lax.fori_loop(STEP * group, STEP * (group + 2), lambda lon, total: total + terms[lon], zero)
 
     arrive(near_all)
     lax.fori_loop(0, 2, lambda i, c: term(1 + final * i, c), 0)
     arrive(far_head[1], far_tail[1])
     term(2, 0)
-    total = opening(1)
+    total = opening(terms, 1)
     corner = final // 2 + 1
     for g in range(2, final):
         arrive(far_head[g], far_tail[g])
         term(g + 1, 0)
-        total = results(g - 1, total)
+        if g - 1 < groups - LATE:
+            total = results(terms, done, g - 1, 0, total)
         if g == corner:
-            arrive(near_west, near_east, east_head, west_head, east_tail, west_tail)
-            lax.fori_loop(0, 2, lambda i, c: term((groups + 1) * i, c), 0)
-            results(0, opening(0))
-    for g in range(final - 1, groups):
-        total = results(g, total)
+            arrive(east_head, west_head, east_tail, west_tail)
+
+            @pl.when(plane != 0)
+            def _():
+                arrive(near_west)
+                term(0, 0)
+
+            @pl.when(plane != PLANES - 1)
+            def _():
+                arrive(near_east)
+                term(groups + 1, 0)
+
+            @pl.when(ends)
+            def _():
+                arrive(*sides)
+                wrap_term((groups + 1) * wrapped)
+
+            results(terms, done, 0, 0, opening(terms, 0))
 
     def finish(*copies):
         for copy in copies:
@@ -276,23 +382,27 @@
 
     each_plane(east_pass, west_pass, finish)
 
-    @pl.when(plane == PLANES - 1)
-    def _():
-        finish(*east_part)
+    @pl.when(eastmost)
+    def _():
+        finish(*east_part, *east_wrap)
 
     @pl.when(plane != PLANES - 1)
     def _():
-        finish(to_east)
+        finish(to_east, near_east)
 
     @pl.when(plane == 0)
     def _():
-        finish(*west_part)
+        finish(*west_part, *west_wrap)
 
     @pl.when(plane != 0)
     def _():
-        finish(to_west)
-
-    for copy in (near_all, near_west, near_east, east_head, west_head, east_tail, west_tail):
+        finish(to_west, near_west)
+
+    @pl.when(ends)
+    def _():
+        finish(*sides)
+
+    for copy in (near_all, east_head, west_head, east_tail, west_tail):
         copy.wait_send()
     for copy in far_head + far_tail:
         copy.wait_send()
@@ -305,22 +415,27 @@
         rows, count, columns = field.shape
         groups = count // STEP
         wide = count + 2 * STEP
-        slots = 10 + 2 * groups + RELAYS
-        result = pl.pallas_call(
+        slots = 16 + 2 * groups + RELAYS
+        wrap_edges = [(STEP, TILE, columns), (PACKED, columns), (STEP, TILE, columns)]
+        done, terms = pl.pallas_call(
             functools.partial(kernel, lons, days),
-            out_shape=pltpu.VMEM((count, rows, columns), jnp.float32),
+            out_shape=(
+                pltpu.VMEM((count - LATE * STEP, rows, columns), jnp.float32),
+                pltpu.VMEM((wide, rows, columns), jnp.float32),
+            ),
             in_specs=[pl.BlockSpec(memory_space=pltpu.HBM)],
-            out_specs=pl.BlockSpec(memory_space=pltpu.VMEM),
+            out_specs=(pl.BlockSpec(memory_space=pltpu.VMEM), pl.BlockSpec(memory_space=pltpu.VMEM)),
             scratch_shapes=[
                 pltpu.VMEM((wide, rows, columns), jnp.bfloat16),
                 pltpu.VMEM((wide, rows, columns), jnp.bfloat16),
                 pltpu.VMEM((wide, TILE, columns), jnp.bfloat16),
                 pltpu.VMEM((groups + 2, PACKED, columns), jnp.bfloat16),
                 pltpu.VMEM((groups, PACKED, columns), jnp.bfloat16),
-                pltpu.VMEM((wide, rows, columns), jnp.float32),
-                pltpu.VMEM((5, rows, PACKED), jnp.bfloat16),
-                pltpu.VMEM((SHARE, rows, columns), jnp.bfloat16),
+                pltpu.VMEM((13, rows, PACKED), jnp.bfloat16),
+                pltpu.VMEM((SHARE, TILE, columns), jnp.bfloat16),
                 pltpu.SemaphoreType.REGULAR((5,)),
+                pltpu.VMEM((STEP, TILE, columns), jnp.bfloat16),
+                *[pltpu.VMEM(edge, jnp.bfloat16) for edge in 2 * wrap_edges],
                 pltpu.SemaphoreType.DMA,
                 pltpu.SemaphoreType.DMA((slots,)),
                 pltpu.SemaphoreType.DMA((slots,)),
@@ -330,6 +445,18 @@
             ),
             name="anomaly",
         )(jnp.transpose(field, (1, 0, 2)))
+        result = pl.pallas_call(
+            finishing,
+            out_shape=jax.ShapeDtypeStruct((count, rows, columns), jnp.float32),
+            in_specs=[pl.BlockSpec(memory_space=pltpu.VMEM)] * 2,
+            out_specs=pl.BlockSpec(memory_space=pl.ANY),
+            scratch_shapes=[
+                pltpu.VMEM((LATE * STEP, rows, columns), jnp.float32),
+                pltpu.SemaphoreType.DMA((groups,)),
+            ],
+            compiler_params=pltpu.CompilerParams(vmem_limit_bytes=24 * 1024 * 1024),
+            name="finishing",
+        )(done, terms)
         return jnp.transpose(result, (1, 0, 2))
 
     return jax.shard_map(

time: 73.3 us -> 72.1 us (0.984)
  local copies, waits for them, and re-layouts: 3.55 us -> 0 us
  Pallas kernels: 69.6 us -> 72 us
    unnamed x1 -> x0, local copies, waits for them, and re-layouts: 3.55 us -> none
    pallas_call x1 -> x2, Pallas kernels: 69.6 us -> 72 us  [the longest x1 68.5 us: local(): pl.pallas_call(functools.partial(kernel, lons, days), out_shape=(pltpu.VM...]
where the time goes in v4:
time: 72.1 us; the launch traced here: 72 us
  Pallas kernels  72 us (100%)
    pallas_call x1, Pallas kernels, local(): pl.pallas_call(functools.partial(kernel, lons, days), out_shape=(pltpu.VM...  68.5 us
    pallas_call x1, Pallas kernels, local(): pl.pallas_call(finishing, out_shape=jax.ShapeDtypeStruct((count, rows, co...  3.53 us

profile of v4, /device:TPU:225, one launch (start us, length us, event | category | flops | bytes accessed | tf_op | source)
XLA Modules:
  0.0 72.0 jit_solution(637527815362565778)
XLA Ops:
  0.0 68.5 %anomaly.1 = (f32[60,23,1024]{2,1,0:T(8,128)S(1)}, f32[110,23,1024]{2,1,0:T(8,128)S(1)}) custom-call(bf16[90,23,1024]{2,1,0:T(8,128)(2,1)} %bitcast.2), custom_call_target="tpu_custom_call" | custom-call | tf_op jit(solution)/shard_map/anomaly/pallas_call | solution.py:420
  68.5 3.5 %finishing.1 = f32[90,23,1024]{2,1,0:T(8,128)} custom-call(f32[60,23,1024]{2,1,0:T(8,128)S(1)} %get-tuple-element.7.done, f32[110,23,1024]{2,1,0:T(8,128)S(1)} %get-tuple-element.8.terms), custom_call_target="tpu_custom_call" | custom-call | tf_op jit(solution)/shard_map/finishing/pallas_call | solution.py:448

commit v5 on v4

--- a/solution.py
+++ b/solution.py
@@ -14,6 +14,7 @@
 REST = DAY_HALF - TILE
 STEP = LON_HALF
 PACKED = (STEP - 1) * TILE
+SCALE = 1.0 / ((2 * DAY_HALF + 1) * (2 * LON_HALF + 1))
 RELAYS = 3
 LATE = 3
 SHARE = 3
@@ -21,12 +22,28 @@
 MESH = pl.DeviceIdType.MESH
 
 
+def product(weights, which, columns, values):
+    return jnp.dot(weights[which, :, 0:columns], values, preferred_element_type=jnp.float32)
+
+
+def strips(weights, first, tail, j):
+    if j < STEP - 1:
+        return product(weights, first, TILE, tail[TILE * j : TILE * (j + 1), :])
+    return product(weights, first + 1, PACKED, tail[...])
+
+
+def group_terms(group, weights, own, near, heads, tails, terms):
+    block = own.shape[1]
+    for j in range(STEP):
+        lon = STEP * group + j
+        total = product(weights, 0, block, own[lon]) + product(weights, 1, block, near[lon])
+        terms[lon] = total + product(weights, 2, TILE, heads[lon]) + strips(weights, 3, tails.at[group], j)
+
+
 def results(terms, target, group, first, total):
-    scale = 1.0 / ((2 * DAY_HALF + 1) * (2 * LON_HALF + 1))
-
     def result(lon, total):
         total = total + terms[lon + 2 * STEP]
-        target[lon - STEP * first] = total * scale
+        target[lon - STEP * first] = total * SCALE
         return total - terms[lon]
 
     return lax.fori_loop(STEP * group, STEP * (group + 1), result, total)
@@ -37,7 +54,7 @@
     return lax.fori_loop(STEP * group, STEP * (group + 2), lambda lon, total: total + terms[lon], zero)
 
 
-def finishing(done, terms, out, late, sems):
+def finishing(done, terms, heads, tails, weights, out, fresh, late, sems):
     early = done.shape[0] // STEP
 
     def put(source, group, first):
@@ -48,9 +65,20 @@
     copies = [put(done, group, 0) for group in range(early)]
     for copy in copies:
         copy.start()
-    total = opening(terms, early)
+    zero = jnp.zeros(terms.shape[1:], jnp.float32)
+    total = lax.fori_loop(STEP * early, STEP * (early + 2), lambda lon, total: total + terms[lon], zero)
+    for j in range(STEP):
+        far = product(weights, 2, TILE, heads[j]) + strips(weights, 3, tails, j)
+        fresh[j] = terms[STEP * (early + 2) + j] + far
     for group in range(early, early + LATE):
-        total = results(terms, late, group, early, total)
+
+        def result(i, total):
+            lon = STEP * group + i
+            total = total + (fresh[i] if group == early else terms[lon + 2 * STEP])
+            late[lon - STEP * early] = total * SCALE
+            return total - (fresh[i] if group == early + 2 else terms[lon])
+
+        total = lax.fori_loop(0, STEP, result, total)
         copies.append(put(late, group, early))
         copies[-1].start()
     for copy in copies:
@@ -58,7 +86,7 @@
 
 
 def kernel(
-    lons, days, field, done, terms, own, near, heads, tails, packed, weights, relayed, ready,
+    lons, days, field, done, terms, last_heads, last_tails, weights, own, near, heads, tails, packed, relayed, ready,
     apart, wrap_heads, wrap_tails, wrap_rests, side_heads, side_tails, side_rests, local_sem, send, recv,
 ):
     count = field.shape[0]
@@ -96,13 +124,11 @@
             greet, (west, day), (west, far_day), *[(level(k), day) for k in reach[1:]], *[(level(-k - 1), day) for k in reach]
         )
     )
-    for k in reach:
-        at(k)()(functools.partial(greet, (level(-k - 1), day)))
     for k in reach[1:]:
         at(PLANES - 1 - k)()(functools.partial(greet, (level(k), day)))
     load = pltpu.make_async_copy(field, own.at[pl.ds(STEP, count)], local_sem)
     load.start()
-    waits = {0: 2, 1: 3, PLANES - 1: 4 + 2 * RELAYS}
+    waits = {0: 2, 1: 3, PLANES - 1: 4 + RELAYS}
     for spot in range(PLANES):
         at(spot)()(functools.partial(pl.semaphore_wait, barrier, waits.get(spot, 4)))
 
@@ -120,6 +146,7 @@
 
     for k in reach:
         at(PLANES - 1 - k)()(functools.partial(tell, 4, (level(k + 1), day)))
+        at(k)()(functools.partial(tell, 5, (level(-k), day)))
 
     def remote(source, target, slot, device, sent=None):
         return pltpu.make_async_remote_copy(
@@ -185,9 +212,15 @@
             pl.when(plane == PLANES - 1 - k)(functools.partial(act, westward[k - 1]))
 
     far_head = [
-        remote(field.at[span(g), head_rows], heads.at[span(g + 1)], 9 + g, (here, far_day)) for g in range(groups)
+        remote(
+            field.at[span(g), head_rows], last_heads if g == final - 1 else heads.at[span(g + 1)], 9 + g, (here, far_day)
+        )
+        for g in range(groups)
     ]
-    far_tail = [remote(packed.at[g], tails.at[g + 1], 9 + groups + g, (here, far_day)) for g in range(groups)]
+    far_tail = [
+        remote(packed.at[g], last_tails if g == final - 1 else tails.at[g + 1], 9 + groups + g, (here, far_day))
+        for g in range(groups)
+    ]
 
     start(far_head[0], far_head[final])
 
@@ -235,7 +268,7 @@
 
     @pl.when(eastmost)
     def _():
-        start(*east_part, east_tail_direct)
+        start(east_part[0], east_tail_direct)
 
     for g in range(1, final):
         start(far_head[g], far_tail[g])
@@ -247,9 +280,17 @@
 
     @pl.when(plane == 0)
     def _():
-        for slot, count_of in ((1, 1), (2, 1), (4, RELAYS)):
-            pl.semaphore_wait(ready.at[slot], count_of)
+        pl.semaphore_wait(ready.at[1], 1)
+        pl.semaphore_wait(ready.at[5], RELAYS)
+        tell(6, (west, day))
+        pl.semaphore_wait(ready.at[2], 1)
+        pl.semaphore_wait(ready.at[4], RELAYS)
         start(*west_part, west_head_direct, west_tail_direct)
+
+    @pl.when(eastmost)
+    def _():
+        pl.semaphore_wait(ready.at[6], 1)
+        start(*east_part[1:])
 
     for k in reach[1:]:
         at(PLANES - 1 - k)()(functools.partial(pl.semaphore_wait, ready.at[3], 1))
@@ -322,19 +363,10 @@
                 peak = jnp.where((position == day_of) & valid, center * (2.0 * DAY_HALF + 1.0), 0.0)
                 weights[5 + 4 * i + n] = (window(position, valid) + peak).astype(jnp.bfloat16)
 
-    def dot(which, columns, values):
-        return jnp.dot(weights[which, :, 0:columns], values, preferred_element_type=jnp.float32)
-
-    def strip(first, tail, j):
-        if j < STEP - 1:
-            return dot(first, TILE, tail[TILE * j : TILE * (j + 1), :])
-        return dot(first + 1, PACKED, tail[...])
+    dot, strip = functools.partial(product, weights), functools.partial(strips, weights)
 
     def term(group, _):
-        for j in range(STEP):
-            lon = STEP * group + j
-            total = dot(0, block, own[lon]) + dot(1, block, near[lon])
-            terms[lon] = total + dot(2, TILE, heads[lon]) + strip(3, tails.at[group], j)
+        group_terms(group, weights, own, near, heads, tails, terms)
         return _
 
     def wrap_term(group):
@@ -352,8 +384,13 @@
     total = opening(terms, 1)
     corner = final // 2 + 1
     for g in range(2, final):
-        arrive(far_head[g], far_tail[g])
-        term(g + 1, 0)
+        if g < final - 1:
+            arrive(far_head[g], far_tail[g])
+            term(g + 1, 0)
+        else:
+            for lon in range(STEP * (g + 1), STEP * (g + 2)):
+                terms[lon] = dot(0, block, own[lon]) + dot(1, block, near[lon])
+            arrive(far_head[g], far_tail[g])
         if g - 1 < groups - LATE:
             total = results(terms, done, g - 1, 0, total)
         if g == corner:
@@ -417,23 +454,26 @@
         wide = count + 2 * STEP
         slots = 16 + 2 * groups + RELAYS
         wrap_edges = [(STEP, TILE, columns), (PACKED, columns), (STEP, TILE, columns)]
-        done, terms = pl.pallas_call(
+        vmem = pl.BlockSpec(memory_space=pltpu.VMEM)
+        gathered = pl.pallas_call(
             functools.partial(kernel, lons, days),
             out_shape=(
                 pltpu.VMEM((count - LATE * STEP, rows, columns), jnp.float32),
                 pltpu.VMEM((wide, rows, columns), jnp.float32),
+                pltpu.VMEM((STEP, TILE, columns), jnp.bfloat16),
+                pltpu.VMEM((PACKED, columns), jnp.bfloat16),
+                pltpu.VMEM((13, rows, PACKED), jnp.bfloat16),
             ),
             in_specs=[pl.BlockSpec(memory_space=pltpu.HBM)],
-            out_specs=(pl.BlockSpec(memory_space=pltpu.VMEM), pl.BlockSpec(memory_space=pltpu.VMEM)),
+            out_specs=(vmem,) * 5,
             scratch_shapes=[
                 pltpu.VMEM((wide, rows, columns), jnp.bfloat16),
                 pltpu.VMEM((wide, rows, columns), jnp.bfloat16),
                 pltpu.VMEM((wide, TILE, columns), jnp.bfloat16),
                 pltpu.VMEM((groups + 2, PACKED, columns), jnp.bfloat16),
                 pltpu.VMEM((groups, PACKED, columns), jnp.bfloat16),
-                pltpu.VMEM((13, rows, PACKED), jnp.bfloat16),
                 pltpu.VMEM((SHARE, TILE, columns), jnp.bfloat16),
-                pltpu.SemaphoreType.REGULAR((5,)),
+                pltpu.SemaphoreType.REGULAR((7,)),
                 pltpu.VMEM((STEP, TILE, columns), jnp.bfloat16),
                 *[pltpu.VMEM(edge, jnp.bfloat16) for edge in 2 * wrap_edges],
                 pltpu.SemaphoreType.DMA,
@@ -441,22 +481,23 @@
                 pltpu.SemaphoreType.DMA((slots,)),
             ],
             compiler_params=pltpu.CompilerParams(
-                collective_id=0, has_side_effects=True, vmem_limit_bytes=44 * 1024 * 1024
+                collective_id=0, has_side_effects=True, vmem_limit_bytes=40 * 1024 * 1024
             ),
             name="anomaly",
         )(jnp.transpose(field, (1, 0, 2)))
         result = pl.pallas_call(
             finishing,
             out_shape=jax.ShapeDtypeStruct((count, rows, columns), jnp.float32),
-            in_specs=[pl.BlockSpec(memory_space=pltpu.VMEM)] * 2,
+            in_specs=[vmem] * 5,
             out_specs=pl.BlockSpec(memory_space=pl.ANY),
             scratch_shapes=[
+                pltpu.VMEM((STEP, rows, columns), jnp.float32),
                 pltpu.VMEM((LATE * STEP, rows, columns), jnp.float32),
                 pltpu.SemaphoreType.DMA((groups,)),
             ],
-            compiler_params=pltpu.CompilerParams(vmem_limit_bytes=24 * 1024 * 1024),
+            compiler_params=pltpu.CompilerParams(vmem_limit_bytes=16 * 1024 * 1024),
             name="finishing",
-        )(done, terms)
+        )(*gathered)
         return jnp.transpose(result, (1, 0, 2))
 
     return jax.shard_map(

time: 72.1 us -> 70 us (0.971)
  the two profiles are of different devices: /device:TPU:225 before, /device:TPU:1 now
where the time goes in v5:
time: 70 us; the launch traced here: 68.9 us
  Pallas kernels  68.9 us (98%)
    pallas_call x1, Pallas kernels, local(): pl.pallas_call(functools.partial(kernel, lons, days), out_shape=(pltpu.VM...  65.4 us
    pallas_call x1, Pallas kernels, local(): pl.pallas_call(finishing, out_shape=jax.ShapeDtypeStruct((count, rows, co...  3.53 us

profile of v5, /device:TPU:1, one launch (start us, length us, event | category | flops | bytes accessed | tf_op | source)
XLA Modules:
  0.0 68.9 jit_solution(5985444295355008649)
XLA Ops:
  0.0 65.4 %anomaly.1 = (f32[60,23,1024]{2,1,0:T(8,128)S(1)}, f32[110,23,1024]{2,1,0:T(8,128)S(1)}, bf16[10,8,1024]{2,1,0:T(8,128)(2,1)S(1)}, bf16[72,1024]{1,0:T(8,128)(2,1)S(1)}, bf16[13,23,72]{2,1,0:T(8,128)(2,1)S(1)}) custom-call(bf16[90,23,1024]{2,1,0:T(8,128)(2,1)} %bitcast.2), custom_call_target="tpu_custom_call" | custom-call | tf_op jit(solution)/shard_map/anomaly/pallas_call | solution.py:458
  65.4 3.5 %finishing.1 = f32[90,23,1024]{2,1,0:T(8,128)} custom-call(f32[60,23,1024]{2,1,0:T(8,128)S(1)} %get-tuple-element.10.done, f32[110,23,1024]{2,1,0:T(8,128)S(1)} %get-tuple-element.11.terms, bf16[10,8,1024]{2,1,0:T(8,128)(2,1)S(1)} %get-tuple-element.12.heads, bf16[72,1024]{1,0:T(8,128)(2,1)S(1)} %get-tuple-element.13.tails, ...), custom_call_target="tpu_custom_call" | custom-call | tf_op jit(solution)/shard_map/finishing/pallas_call | solution.py:488

commit v6 on v5

--- a/solution.py
+++ b/solution.py
@@ -14,6 +14,7 @@
 REST = DAY_HALF - TILE
 STEP = LON_HALF
 PACKED = (STEP - 1) * TILE
+DENSE = REST * TILE
 SCALE = 1.0 / ((2 * DAY_HALF + 1) * (2 * LON_HALF + 1))
 RELAYS = 3
 LATE = 3
@@ -32,12 +33,18 @@
     return product(weights, first + 1, PACKED, tail[...])
 
 
-def group_terms(group, weights, own, near, heads, tails, terms):
+def group_terms(group, weights, own, near, heads, tails, terms, moved=None):
     block = own.shape[1]
     for j in range(STEP):
         lon = STEP * group + j
         total = product(weights, 0, block, own[lon]) + product(weights, 1, block, near[lon])
-        terms[lon] = total + product(weights, 2, TILE, heads[lon]) + strips(weights, 3, tails.at[group], j)
+        total += product(weights, 2, TILE, heads[lon])
+        if moved is None or j < REST:
+            total += strips(weights, 3, tails.at[group], j)
+        else:
+            rows = tails[group, 0:DENSE, :] if j == STEP - 1 else moved[j - REST]
+            total += product(weights, 4, DENSE, rows)
+        terms[lon] = total
 
 
 def results(terms, target, group, first, total):
@@ -86,7 +93,7 @@
 
 
 def kernel(
-    lons, days, field, done, terms, last_heads, last_tails, weights, own, near, heads, tails, packed, relayed, ready,
+    lons, days, field, done, terms, last_heads, last_tails, weights, own, near, heads, tails, packed, strayed, moved, relayed, ready,
     apart, wrap_heads, wrap_tails, wrap_rests, side_heads, side_tails, side_rests, local_sem, send, recv,
 ):
     count = field.shape[0]
@@ -167,6 +174,8 @@
 
     head_rows = pl.ds(pl.multiple_of(TILE * core, TILE), TILE)
     final = groups - 1
+    thin = final - 2
+    holders = (0, final, *range(1, REST - 1))
 
     to_east = remote(field.at[span(final)], own.at[span(0)], 0, (east, day))
     to_west = remote(field.at[span(0)], own.at[span(groups + 1)], 1, (west, day))
@@ -218,7 +227,11 @@
         for g in range(groups)
     ]
     far_tail = [
-        remote(packed.at[g], last_tails if g == final - 1 else tails.at[g + 1], 9 + groups + g, (here, far_day))
+        remote(
+            packed.at[g, pl.ds(0, DENSE)] if g == thin else packed.at[g],
+            last_tails if g == final - 1 else tails.at[g + 1, pl.ds(0, DENSE)] if g == thin else tails.at[g + 1],
+            9 + groups + g, (here, far_day),
+        )
         for g in range(groups)
     ]
 
@@ -239,11 +252,15 @@
         rows = pl.ds(pl.multiple_of(TILE + TILE * core, TILE), REST)
         return own[lon, rows, :].astype(jnp.float32)
 
+    for i in range(STEP - 1 - REST):
+        strayed[i, 0:REST, :] = rest(STEP * (thin + 1) + REST + i)
+
     def pack(group, _):
         base = STEP * (group + 1)
         spare = rest(base + STEP - 1)
+        row = jnp.where(group == 0, 0, jnp.where(group == final, 1, jnp.minimum(group + 1, REST - 1)))
         for j in range(STEP - 1):
-            extra = spare[j % REST : j % REST + 1]
+            extra = spare[j : j + 1] if j < REST else strayed[j - REST, pl.ds(row, 1), :]
             tile = jnp.concatenate([rest(base + j), extra], axis=0)
             packed[group, TILE * j : TILE * (j + 1), :] = tile.astype(jnp.bfloat16)
         return _
@@ -386,7 +403,14 @@
     for g in range(2, final):
         if g < final - 1:
             arrive(far_head[g], far_tail[g])
-            term(g + 1, 0)
+            if g == thin:
+                for i in range(STEP - 1 - REST):
+                    place_in = pl.ds(TILE * (REST + i), TILE)
+                    for n, holder in enumerate(holders):
+                        moved[i, TILE * n : TILE * (n + 1), :] = tails[holder + 1, place_in, :]
+                group_terms(g + 1, weights, own, near, heads, tails, terms, moved)
+            else:
+                term(g + 1, 0)
         else:
             for lon in range(STEP * (g + 1), STEP * (g + 2)):
                 terms[lon] = dot(0, block, own[lon]) + dot(1, block, near[lon])
@@ -472,6 +496,8 @@
                 pltpu.VMEM((wide, TILE, columns), jnp.bfloat16),
                 pltpu.VMEM((groups + 2, PACKED, columns), jnp.bfloat16),
                 pltpu.VMEM((groups, PACKED, columns), jnp.bfloat16),
+                pltpu.VMEM((STEP - 1 - REST, TILE, columns), jnp.float32),
+                pltpu.VMEM((STEP - 1 - REST, DENSE, columns), jnp.bfloat16),
                 pltpu.VMEM((SHARE, TILE, columns), jnp.bfloat16),
                 pltpu.SemaphoreType.REGULAR((7,)),
                 pltpu.VMEM((STEP, TILE, columns), jnp.bfloat16),

time: 70 us -> 69.3 us (0.990)
  Pallas kernels: 68.9 us -> 68.2 us
    pallas_call x1, Pallas kernels: 65.4 us -> 64.7 us  [local(): pl.pallas_call(functools.partial(kernel, lons, days), out_shape=(pltpu.VM...]
where the time goes in v6:
time: 69.3 us; the launch traced here: 68.2 us
  Pallas kernels  68.2 us (98%)
    pallas_call x1, Pallas kernels, local(): pl.pallas_call(functools.partial(kernel, lons, days), out_shape=(pltpu.VM...  64.7 us
    pallas_call x1, Pallas kernels, local(): pl.pallas_call(finishing, out_shape=jax.ShapeDtypeStruct((count, rows, co...  3.53 us

profile of v6, /device:TPU:1, one launch (start us, length us, event | category | flops | bytes accessed | tf_op | source)
XLA Modules:
  0.0 68.2 jit_solution(15258605730879758806)
XLA Ops:
  0.0 64.7 %anomaly.1 = (f32[60,23,1024]{2,1,0:T(8,128)S(1)}, f32[110,23,1024]{2,1,0:T(8,128)S(1)}, bf16[10,8,1024]{2,1,0:T(8,128)(2,1)S(1)}, bf16[72,1024]{1,0:T(8,128)(2,1)S(1)}, bf16[13,23,72]{2,1,0:T(8,128)(2,1)S(1)}) custom-call(bf16[90,23,1024]{2,1,0:T(8,128)(2,1)} %bitcast.2), custom_call_target="tpu_custom_call" | custom-call | tf_op jit(solution)/shard_map/anomaly/pallas_call | solution.py:482
  64.7 3.5 %finishing.1 = f32[90,23,1024]{2,1,0:T(8,128)} custom-call(f32[60,23,1024]{2,1,0:T(8,128)S(1)} %get-tuple-element.10.done, f32[110,23,1024]{2,1,0:T(8,128)S(1)} %get-tuple-element.11.terms, bf16[10,8,1024]{2,1,0:T(8,128)(2,1)S(1)} %get-tuple-element.12.heads, bf16[72,1024]{1,0:T(8,128)(2,1)S(1)} %get-tuple-element.13.tails, ...), custom_call_target="tpu_custom_call" | custom-call | tf_op jit(solution)/shard_map/finishing/pallas_call | solution.py:514

commit v7 on v6

--- a/solution.py
+++ b/solution.py
@@ -128,16 +128,16 @@
     pl.when(plane != PLANES - 1)(functools.partial(greet, (east, day)))
     at(0)()(
         functools.partial(
-            greet, (west, day), (west, far_day), *[(level(k), day) for k in reach[1:]], *[(level(-k - 1), day) for k in reach]
+            greet, (west, day), *[(level(k), day) for k in reach[1:]]
         )
     )
     for k in reach[1:]:
         at(PLANES - 1 - k)()(functools.partial(greet, (level(k), day)))
     load = pltpu.make_async_copy(field, own.at[pl.ds(STEP, count)], local_sem)
     load.start()
-    waits = {0: 2, 1: 3, PLANES - 1: 4 + RELAYS}
+    waits = {0: 2, **{k: 4 for k in reach[1:]}, PLANES - 1: 3 + RELAYS}
     for spot in range(PLANES):
-        at(spot)()(functools.partial(pl.semaphore_wait, barrier, waits.get(spot, 4)))
+        at(spot)()(functools.partial(pl.semaphore_wait, barrier, waits.get(spot, 3)))
 
     def tell(slot, *partners):
         for partner in partners:
@@ -148,12 +148,10 @@
     @pl.when(eastmost)
     def _():
         tell(1, (east, day))
-        tell(2, (east, far_day))
-        tell(3, *[(level(-k), day) for k in reach[1:]])
+        tell(2, *[(level(-k), day) for k in reach[1:]])
 
     for k in reach:
-        at(PLANES - 1 - k)()(functools.partial(tell, 4, (level(k + 1), day)))
-        at(k)()(functools.partial(tell, 5, (level(-k), day)))
+        at(k)()(functools.partial(tell, 3, (level(-k), day)))
 
     def remote(source, target, slot, device, sent=None):
         return pltpu.make_async_remote_copy(
@@ -237,10 +235,6 @@
 
     start(far_head[0], far_head[final])
 
-    @pl.when(eastmost)
-    def _():
-        start(east_head_direct)
-
     @pl.when(plane != 0)
     def _():
         start(to_west)
@@ -285,7 +279,7 @@
 
     @pl.when(eastmost)
     def _():
-        start(east_part[0], east_tail_direct)
+        start(east_part[0])
 
     for g in range(1, final):
         start(far_head[g], far_tail[g])
@@ -298,19 +292,17 @@
     @pl.when(plane == 0)
     def _():
         pl.semaphore_wait(ready.at[1], 1)
-        pl.semaphore_wait(ready.at[5], RELAYS)
-        tell(6, (west, day))
-        pl.semaphore_wait(ready.at[2], 1)
-        pl.semaphore_wait(ready.at[4], RELAYS)
+        pl.semaphore_wait(ready.at[3], RELAYS)
+        tell(4, (west, day))
         start(*west_part, west_head_direct, west_tail_direct)
 
     @pl.when(eastmost)
     def _():
-        pl.semaphore_wait(ready.at[6], 1)
-        start(*east_part[1:])
+        pl.semaphore_wait(ready.at[4], 1)
+        start(*east_part[1:], east_head_direct, east_tail_direct)
 
     for k in reach[1:]:
-        at(PLANES - 1 - k)()(functools.partial(pl.semaphore_wait, ready.at[3], 1))
+        at(PLANES - 1 - k)()(functools.partial(pl.semaphore_wait, ready.at[2], 1))
 
     def forward(copy):
         arrive(east_part[1])
@@ -499,7 +491,7 @@
                 pltpu.VMEM((STEP - 1 - REST, TILE, columns), jnp.float32),
                 pltpu.VMEM((STEP - 1 - REST, DENSE, columns), jnp.bfloat16),
                 pltpu.VMEM((SHARE, TILE, columns), jnp.bfloat16),
-                pltpu.SemaphoreType.REGULAR((7,)),
+                pltpu.SemaphoreType.REGULAR((5,)),
                 pltpu.VMEM((STEP, TILE, columns), jnp.bfloat16),
                 *[pltpu.VMEM(edge, jnp.bfloat16) for edge in 2 * wrap_edges],
                 pltpu.SemaphoreType.DMA,

time: 69.3 us -> 69.3 us (level)
  no operation moved by 1% of the time
where the time goes in v7:
time: 69.3 us; the launch traced here: 68.2 us
  Pallas kernels  68.2 us (98%)
    pallas_call x1, Pallas kernels, local(): pl.pallas_call(functools.partial(kernel, lons, days), out_shape=(pltpu.VM...  64.6 us
    pallas_call x1, Pallas kernels, local(): pl.pallas_call(finishing, out_shape=jax.ShapeDtypeStruct((count, rows, co...  3.53 us

profile of v7, /device:TPU:1, one launch (start us, length us, event | category | flops | bytes accessed | tf_op | source)
XLA Modules:
  0.0 68.2 jit_solution(9629079566218952173)
XLA Ops:
  0.0 64.6 %anomaly.1 = (f32[60,23,1024]{2,1,0:T(8,128)S(1)}, f32[110,23,1024]{2,1,0:T(8,128)S(1)}, bf16[10,8,1024]{2,1,0:T(8,128)(2,1)S(1)}, bf16[72,1024]{1,0:T(8,128)(2,1)S(1)}, bf16[13,23,72]{2,1,0:T(8,128)(2,1)S(1)}) custom-call(bf16[90,23,1024]{2,1,0:T(8,128)(2,1)} %bitcast.2), custom_call_target="tpu_custom_call" | custom-call | tf_op jit(solution)/shard_map/anomaly/pallas_call | solution.py:474
  64.6 3.5 %finishing.1 = f32[90,23,1024]{2,1,0:T(8,128)} custom-call(f32[60,23,1024]{2,1,0:T(8,128)S(1)} %get-tuple-element.10.done, f32[110,23,1024]{2,1,0:T(8,128)S(1)} %get-tuple-element.11.terms, bf16[10,8,1024]{2,1,0:T(8,128)(2,1)S(1)} %get-tuple-element.12.heads, bf16[72,1024]{1,0:T(8,128)(2,1)S(1)} %get-tuple-element.13.tails, ...), custom_call_target="tpu_custom_call" | custom-call | tf_op jit(solution)/shard_map/finishing/pallas_call | solution.py:506

commit v8 on v7

--- a/solution.py
+++ b/solution.py
@@ -249,7 +249,8 @@
     for i in range(STEP - 1 - REST):
         strayed[i, 0:REST, :] = rest(STEP * (thin + 1) + REST + i)
 
-    def pack(group, _):
+    def pack(turn_of, _):
+        group = lax.rem(turn_of + final, groups)
         base = STEP * (group + 1)
         spare = rest(base + STEP - 1)
         row = jnp.where(group == 0, 0, jnp.where(group == final, 1, jnp.minimum(group + 1, REST - 1)))
@@ -277,12 +278,12 @@
 
     start(far_tail[0], far_tail[final])
 
-    @pl.when(eastmost)
-    def _():
-        start(east_part[0])
-
     for g in range(1, final):
         start(far_head[g], far_tail[g])
+
+    @pl.when(eastmost)
+    def _():
+        start(east_part[0])
 
     @pl.when(plane != PLANES - 1)
     def _():

time: 69.3 us -> 69.3 us (level)
  no operation moved by 1% of the time
where the time goes in v8:
time: 69.3 us; the launch traced here: 68.2 us
  Pallas kernels  68.2 us (98%)
    pallas_call x1, Pallas kernels, local(): pl.pallas_call(functools.partial(kernel, lons, days), out_shape=(pltpu.VM...  64.6 us
    pallas_call x1, Pallas kernels, local(): pl.pallas_call(finishing, out_shape=jax.ShapeDtypeStruct((count, rows, co...  3.53 us

profile of v8, /device:TPU:1, one launch (start us, length us, event | category | flops | bytes accessed | tf_op | source)
XLA Modules:
  0.0 68.2 jit_solution(7063798735607086190)
XLA Ops:
  0.0 64.6 %anomaly.1 = (f32[60,23,1024]{2,1,0:T(8,128)S(1)}, f32[110,23,1024]{2,1,0:T(8,128)S(1)}, bf16[10,8,1024]{2,1,0:T(8,128)(2,1)S(1)}, bf16[72,1024]{1,0:T(8,128)(2,1)S(1)}, bf16[13,23,72]{2,1,0:T(8,128)(2,1)S(1)}) custom-call(bf16[90,23,1024]{2,1,0:T(8,128)(2,1)} %bitcast.2), custom_call_target="tpu_custom_call" | custom-call | tf_op jit(solution)/shard_map/anomaly/pallas_call | solution.py:475
  64.6 3.5 %finishing.1 = f32[90,23,1024]{2,1,0:T(8,128)} custom-call(f32[60,23,1024]{2,1,0:T(8,128)S(1)} %get-tuple-element.10.done, f32[110,23,1024]{2,1,0:T(8,128)S(1)} %get-tuple-element.11.terms, bf16[10,8,1024]{2,1,0:T(8,128)(2,1)S(1)} %get-tuple-element.12.heads, bf16[72,1024]{1,0:T(8,128)(2,1)S(1)} %get-tuple-element.13.tails, ...), custom_call_target="tpu_custom_call" | custom-call | tf_op jit(solution)/shard_map/finishing/pallas_call | solution.py:507
